TPU v7x, 8 devices: a whole 2x2x1 slice. The times are simulated.
8 devices in a mesh: kv: 2 (over z, y), dup: 4 (over x, core).
Axes of the slice: x: 2, y: 2, z: 1, core: 2. Of those that a mesh axis runs over, the one named last changes fastest.
Arguments:
- queries: bfloat16 [512, 32, 128], P('kv', 'dup'), parts along dimension 0
- key_cache: bfloat16 [512, 2048, 128], P('kv', 'dup'), parts along dimension 0
- value_cache: bfloat16 [512, 2048, 128], P('kv', 'dup'), parts along dimension 0
- lengths: int32 [512], P('kv'), parts along dimension 0
Outputs:
- output: bfloat16 [512, 32, 128], P('kv', 'dup'), parts along dimension 0
There are 2 independent parts. A program takes and returns all parts, laid end to end along the dimension named above; each array names one.
All inputs are finite; a program needn't handle non-finite values.
Results may differ from a plain program's by a relative error of at most 0.0071394.
Values are sent between devices in bfloat16 or wider.
A program may use at most 1 GiB of HBM per device.

v0:
```python
import jax
import jax.numpy as jnp
from jax import lax
from jax.sharding import PartitionSpec as P, NamedSharding

DRAFT = 4
NEG_BIG = -1e30


def solution(mesh):
    dup_size = mesh.shape["dup"]

    def group_step(q_local, k_span, v_span, len_local):
        num_batch, span_len, head_dim = k_span.shape
        span_start = lax.axis_index("dup") * span_len
        q_group = lax.all_gather(q_local, "dup", axis=1, tiled=True)
        num_rows = q_group.shape[1]
        own_rows = num_rows // dup_size
        scores = jnp.einsum("brd,bsd->brs", q_group, k_span, preferred_element_type=jnp.float32) * (head_dim ** -0.5)
        last_pos = len_local[:, None] - DRAFT + (jnp.arange(num_rows) % DRAFT)[None, :]
        allowed = (span_start + jnp.arange(span_len))[None, None, :] <= last_pos[:, :, None]
        scores = jnp.where(allowed, scores, NEG_BIG)
        row_peak = jnp.max(scores, axis=2, keepdims=True)
        prob_vals = jnp.exp(scores - row_peak)
        row_mass = jnp.sum(prob_vals, axis=2, keepdims=True)
        weighted = jnp.einsum("brs,bsd->brd", prob_vals.astype(jnp.bfloat16), v_span, preferred_element_type=jnp.float32)
        part_out = (weighted / row_mass).astype(jnp.bfloat16).reshape(num_batch, dup_size, own_rows, head_dim)
        log_mass = (row_peak + jnp.log(row_mass)).reshape(num_batch, dup_size, own_rows)
        recv_out = lax.all_to_all(part_out, "dup", 1, 1)
        recv_mass = lax.all_to_all(log_mass, "dup", 1, 1)
        top_mass = jnp.max(recv_mass, axis=1, keepdims=True)
        weights = jnp.exp(recv_mass - top_mass)
        total_mass = jnp.sum(weights, axis=1)
        merged = jnp.sum(weights[..., None] * recv_out.astype(jnp.float32), axis=1)
        return (merged / total_mass[..., None]).astype(jnp.bfloat16)

    return jax.shard_map(group_step, mesh=mesh, in_specs=(P("kv", "dup", None), P("kv", "dup", None), P("kv", "dup", None), P("kv")), out_specs=P("kv", "dup", None), check_vma=False)
```

profile of v0, /device:TPU:0, one launch (start us, length us, event | category | flops | bytes accessed | tf_op | source)
XLA Modules:
  0.0 129.9 jit_solution(13054711165030936161)
XLA Ops:
  6.5 0.0 all-gather.2.cloned.1.call-start
  6.5 0.7 all-gather.2.cloned.1.call-update
  7.3 0.7 broadcast_add_fusion.1
  8.0 0.1 broadcast_add_fusion
  8.1 23.4 %all-gather.2.cloned.1.call-done = bf16[256,32,128]{2,1,0:T(8,128)(2,1)} async-done(((bf16[256,8,128]{2,1,0:T(8,128)(2,1)}), bf16[256,32,128]{2,1,0:T(8,128)(2,1)}) %all-gather.2.cloned.1.call-update) | async-done | bytes 2097168 | tf_op jit(solution)/shard_map/all_gather | solution.py:16
  31.5 23.4 %fusion.2 = (f32[256,32]{1,0:T(8,128)S(1)}, f32[256,32,512]{2,1,0:T(8,128)}) fusion(s32[256,32]{1,0:T(8,128)S(1)} %broadcast_add_fusion, s32[512]{0:T(512)S(1)} %iota_add_fusion, bf16[256,32,128]{2,1,0:T(8,128)(2,1)} %all-gather.2.cloned.1.call-done, bf16[256,512,128]{2,1,0:T(8,128)(2,1)} %param.5), kind=kOutput, calls=%fused_computation.4 | convolution fusion | flops 1090510848 | bytes 52496384 | tf_op jit(solution)/shard_map/brd,bsd->brs/dot_general | solution.py:19
  54.9 0.1 copy.13
  55.0 12.1 %fusion.1 = f32[256,32]{1,0:T(8,128)S(1)} fusion(f32[256,32,512]{2,1,0:T(8,128)} %get-tuple-element.8, f32[256,32]{1,0:T(8,128)S(1)} %get-tuple-element.7, s32[256,32]{1,0:T(8,128)S(1)} %broadcast_add_fusion, s32[512]{0:T(512)S(1)} %iota_add_fusion), kind=kLoop, calls=%fused_computation.3 | loop fusion | flops 20963328 | bytes 16877568 | tf_op jit(solution)/shard_map/reduce_sum | solution.py:25
  67.1 0.1 copy.12
  67.2 0.6 add_bitcast_fusion
  67.8 3.3 %all-to-all-start = ((f32[256,4,8]{0,2,1:T(8,128)}), f32[256,4,8]{0,2,1:T(8,128)S(1)}, u32[]{:S(2)}, u32[]{:S(2)}) async-start(f32[256,4,8]{0,2,1:T(8,128)} %add_bitcast_fusion), calls=%async_computation | async-start | bytes 65536 | tf_op jit(solution)/shard_map/all_to_all | solution.py:30
  71.1 18.5 %fusion.10 = bf16[256,4,8,128]{3,2,1,0:T(8,128)(2,1)S(1)} fusion(f32[256,32]{1,0:T(8,128)S(1)} %fusion.1, bf16[256,512,128]{2,1,0:T(8,128)(2,1)} %param.6, f32[256,32,512]{2,1,0:T(8,128)} %get-tuple-element.8, f32[256,32]{1,0:T(8,128)S(1)} %get-tuple-element.7, s32[256,32]{1,0:T(8,128)S(1)} %broadcast_add_fusion, s32[512]{0:T(512)S(1)} %iota_add_fusion), kind=kOutput, calls=%fused_computation.13 | convolution fusion | flops 1096810496 | bytes 52529152 | tf_op jit(solution)/shard_map/brs,bsd->brd/dot_general | solution.py:26
  89.6 1.7 %copy.15 = bf16[256,4,8,128]{3,2,0,1:T(8,128)(2,1)} copy(bf16[256,4,8,128]{3,2,1,0:T(8,128)(2,1)S(1)} %fusion.10) | data formatting | bytes 4194304 | tf_op jit(solution)/shard_map/reshape | solution.py:27
  91.3 0.0 all-to-all-done
  91.3 3.6 %all-to-all-start.1 = ((bf16[256,4,8,128]{3,2,0,1:T(8,128)(2,1)}), bf16[256,4,8,128]{3,2,0,1:T(8,128)(2,1)S(1)}, u32[]{:S(2)}, u32[]{:S(2)}) async-start(bf16[256,4,8,128]{3,2,0,1:T(8,128)(2,1)} %copy.15), calls=%async_computation.1 | async-start | bytes 4194304 | tf_op jit(solution)/shard_map/all_to_all | solution.py:29
  94.9 0.2 copy.14
  95.1 0.1 copy.16
  95.3 25.0 %all-to-all-done.1 = bf16[256,4,8,128]{3,2,0,1:T(8,128)(2,1)S(1)} async-done(((bf16[256,4,8,128]{3,2,0,1:T(8,128)(2,1)}), bf16[256,4,8,128]{3,2,0,1:T(8,128)(2,1)S(1)}, u32[]{:S(2)}, u32[]{:S(2)}) %all-to-all-start.1) | async-done | bytes 2097184 | tf_op jit(solution)/shard_map/all_to_all | solution.py:29
  120.3 1.6 %multiply_reduce_fusion = f32[256,8,128]{2,1,0:T(8,128)S(1)} fusion(bf16[256,4,8,128]{3,2,0,1:T(8,128)(2,1)S(1)} %all-to-all-done.1, f32[256,4,8]{2,0,1:T(8,128)S(1)} %copy.14), kind=kLoop, calls=%fused_computation.11 | loop fusion | flops 2883584 | bytes 3178496 | tf_op jit(solution)/shard_map/reduce_sum | solution.py:34
  121.9 1.1 divide_convert_fusion.1
  (4 shorter events, 0.0 us)
Async XLA Ops:
  6.5 25.0 %all-gather.2.cloned.1.call-start = ((), (), s32[]{:S(2)}) async-start(), calls=%async_computation.2 | async-start | bytes 2621440 | tf_op jit(solution)/shard_map/all_gather | solution.py:16
  67.8 23.4 %all-to-all-start = ((f32[256,4,8]{0,2,1:T(8,128)}), f32[256,4,8]{0,2,1:T(8,128)S(1)}, u32[]{:S(2)}, u32[]{:S(2)}) async-start(f32[256,4,8]{0,2,1:T(8,128)} %add_bitcast_fusion), calls=%async_computation | async-start | bytes 65536 | tf_op jit(solution)/shard_map/all_to_all | solution.py:30
  91.3 29.0 %all-to-all-start.1 = ((bf16[256,4,8,128]{3,2,0,1:T(8,128)(2,1)}), bf16[256,4,8,128]{3,2,0,1:T(8,128)(2,1)S(1)}, u32[]{:S(2)}, u32[]{:S(2)}) async-start(bf16[256,4,8,128]{3,2,0,1:T(8,128)(2,1)} %copy.15), calls=%async_computation.1 | async-start | bytes 4194304 | tf_op jit(solution)/shard_map/all_to_all | solution.py:29
Sparse Core Ops, SparseCore 0:
  8.9 22.6 all-gather.1
where the time goes:
time: 130 us
  waiting for transfers between devices  49.2 us (38%)
  matrix products  41.9 us (32%)
  other arithmetic  16.3 us (13%)
  between operations  13.5 us (10%)
  starting transfers between devices  6.87 us (5%)
  local copies, waits for them, and re-layouts  2.17 us (2%)
    all_to_all x1, waiting for transfers between devices, group_step(): recv_out = lax.all_to_all(part_out, 'dup', 1, 1)  25 us
    all_gather x1, waiting for transfers between devices, group_step(): q_group = lax.all_gather(q_local, 'dup', axis=1, tiled=True)  23.4 us
    dot_general x1, matrix products, group_step(): jnp.einsum('brd,bsd->brs', q_group, k_span, preferred_element_type=jnp.fl...  23.4 us
    dot_general x1, matrix products, group_step(): jnp.einsum('brs,bsd->brd', prob_vals.astype(jnp.bfloat16), v_span, prefer...  18.5 us
    reduce_sum x1, other arithmetic, group_step(): row_mass = jnp.sum(prob_vals, axis=2, keepdims=True)  12.1 us
    all_to_all x1, starting transfers between devices, group_step(): recv_out = lax.all_to_all(part_out, 'dup', 1, 1)  3.61 us
    all_to_all x1, starting transfers between devices, group_step(): recv_mass = lax.all_to_all(log_mass, 'dup', 1, 1)  3.26 us
  transfers between devices with their start and end apart: 3, of which 2 were waited for; matrix products, arithmetic and copies ran while one was open for 16% of the time, Pallas kernels for 0%

commit v1 on v0

v1 whole, which is shorter than its diff:
```python
import functools
import math

import jax
import jax.numpy as jnp
from jax import lax
from jax.experimental import pallas as pl
from jax.experimental.pallas import tpu as pltpu
from jax.sharding import PartitionSpec as P

DRAFT = 4
CHUNK = 16
RING = 6
AHEAD = 2
FINAL_LAG = 10
ROWS = 8
MESH = pl.DeviceIdType.MESH
LOWEST = -3.0e38
FLOOR = -2.0e38


def kernel(
    num_chunks,
    scale,
    len_ref,
    q_hbm,
    k_hbm,
    v_hbm,
    out_hbm,
    kbuf,
    vbuf,
    qbuf,
    sbuf,
    part,
    stat,
    peer_part,
    peer_stat,
    send_out,
    send_lse,
    recv_out,
    recv_lse,
    own_lse,
    out_buf,
    k_sem,
    v_sem,
    q_local,
    q_chip_send,
    q_chip_recv,
    q_sib_send,
    q_sib_recv,
    q_fwd_send,
    q_fwd_recv,
    part_send,
    part_recv,
    stat_send,
    stat_recv,
    o_send,
    o_recv,
    l_send,
    l_recv,
    out_sem,
):
    me = lax.axis_index("dup")
    chip, core = me // 2, lax.rem(me, 2)
    sib = 2 * chip + (1 - core)
    far = 2 * (1 - chip) + core
    far_sib = 2 * (1 - chip) + (1 - core)
    span = kbuf.shape[2]
    pairs = CHUNK // 2

    def load_k(step, slot):
        return pltpu.make_async_copy(k_hbm.at[pl.ds(step * CHUNK, CHUNK)], kbuf.at[slot], k_sem.at[slot])

    def load_v(step, slot):
        return pltpu.make_async_copy(v_hbm.at[pl.ds(step * CHUNK, CHUNK)], vbuf.at[slot], v_sem.at[slot])

    def q_rows(step, owner):
        return qbuf.at[pl.ds(step * CHUNK, CHUNK), pl.ds(pl.multiple_of(owner * ROWS, ROWS), ROWS)]

    def q_mine(step):
        return q_hbm.at[pl.ds(step * CHUNK, CHUNK)]

    def keep_q(step):
        return pltpu.make_async_copy(q_mine(step), q_rows(step, me), q_local.at[step])

    def remote(src, dst, send, recv, dev):
        return pltpu.make_async_remote_copy(
            src_ref=src, dst_ref=dst, send_sem=send, recv_sem=recv, device_id={"dup": dev}, device_id_type=MESH
        )

    def q_to_far(step, owner):
        return remote(q_mine(step), q_rows(step, owner), q_chip_send.at[step], q_chip_recv.at[step], far)

    def q_to_sib(step, owner):
        return remote(q_mine(step), q_rows(step, owner), q_sib_send.at[step], q_sib_recv.at[step], sib)

    def q_forward(step, owner):
        return remote(q_rows(step, owner), q_rows(step, owner), q_fwd_send.at[step], q_fwd_recv.at[step], sib)

    def give_part(step):
        return remote(part.at[step, 1 - core], peer_part.at[step], part_send.at[step], part_recv.at[step], sib)

    def give_stat(step):
        return remote(stat.at[step], peer_stat.at[step], stat_send.at[step], stat_recv.at[step], sib)

    def give_out(step):
        return remote(send_out.at[step], recv_out.at[step], o_send.at[step], o_recv.at[step], far)

    def give_lse(step):
        return remote(send_lse.at[step], recv_lse.at[step], l_send.at[step], l_recv.at[step], far)

    def store_out(step):
        return pltpu.make_async_copy(
            out_buf.at[step], out_hbm.at[pl.ds(step * CHUNK * ROWS, CHUNK * ROWS)], out_sem.at[step]
        )

    for step in range(RING):
        load_k(step, step).start()
        load_v(step, step).start()

    barrier = pltpu.get_barrier_semaphore()
    for dev in (sib, far):
        pl.semaphore_signal(barrier, inc=1, device_id={"dup": dev}, device_id_type=MESH)
    pl.semaphore_wait(barrier, 2)

    @pl.loop(0, num_chunks)
    def _(step):
        q_to_far(step, me).start()
        q_to_sib(step, me).start()
        keep_q(step).start()

    def forward_q(step):
        q_to_far(step, far).wait_recv()
        q_forward(step, far).start()

    def await_q(step):
        keep_q(step).wait()
        q_to_sib(step, sib).wait_recv()
        q_forward(step, far_sib).wait_recv()

    lane = lax.broadcasted_iota(jnp.int32, (ROWS, 128), 1)
    draft_of_row = lax.rem(lax.broadcasted_iota(jnp.int32, (ROWS, span), 0), DRAFT)
    reach = lax.broadcasted_iota(jnp.int32, (ROWS, span), 1) - draft_of_row + (me * span + DRAFT)
    log2e = 1.0 / math.log(2.0)
    rate = scale * log2e

    def score_pair(step, slot, at, i):
        b = step * CHUNK + 2 * i
        q_a, q_b = qbuf[b], qbuf[b + 1]
        none = jnp.zeros_like(q_a)
        left = jnp.concatenate([jnp.concatenate([q_a, none], 1), jnp.concatenate([none, q_b], 1)], 0)
        right = jnp.concatenate([kbuf[slot, 2 * i], kbuf[slot, 2 * i + 1]], 1)
        sbuf[at, i] = lax.dot_general(left, right, (((1,), (1,)), ((), ())), preferred_element_type=jnp.float32)

    def attend_pair(step, slot, at, i, peaks, masses):
        probs = []
        for h in range(2):
            allowed = reach <= len_ref[step * CHUNK + 2 * i + h]
            for d in range(4):
                s = sbuf[at, i, pl.ds(32 * h + 8 * d, 8), :]
                s = jnp.where(allowed, s, LOWEST)
                peak = jnp.maximum(jnp.max(s, axis=1, keepdims=True), FLOOR)
                p = jnp.exp2((s - peak) * rate)
                mass = jnp.sum(p, axis=1, keepdims=True)
                here = lane == (CHUNK * d + 2 * i + h)
                peaks = jnp.where(here, peak, peaks)
                masses = jnp.where(here, mass, masses)
                probs.append(p)
        p = jnp.concatenate(probs, 0).astype(jnp.bfloat16)
        v = jnp.concatenate([vbuf[slot, 2 * i], vbuf[slot, 2 * i + 1]], 1)
        o = lax.dot_general(p, v, (((1,), (0,)), ((), ())), preferred_element_type=jnp.float32)
        for h in range(2):
            for d in range(4):
                part[step, d % 2, d // 2, 2 * i + h] = o[32 * h + 8 * d : 32 * h + 8 * d + 8, 128 * h : 128 * h + 128]
        return peaks, masses

    def to_front(tile, owner):
        return pltpu.roll(tile, lax.rem(128 - owner * CHUNK, 128), 1)

    def merge_chip(step):
        m_a, l_a, m_b, l_b = stat[step, 0], stat[step, 1], peer_stat[step, 0], peer_stat[step, 1]
        top = jnp.maximum(m_a, m_b)
        w_a, w_b = jnp.exp2((m_a - top) * rate), jnp.exp2((m_b - top) * rate)
        total = w_a * l_a + w_b * l_b
        some = total > 0.0
        safe = jnp.where(some, total, 1.0)
        inverse = jnp.where(some, 1.0 / safe, 0.0)
        w_a, w_b = w_a * inverse, w_b * inverse
        lse = jnp.where(some, top * rate + jnp.log2(safe), LOWEST)
        own_lse[step] = to_front(lse, me)
        send_lse[step] = to_front(lse, far)
        w_a_own, w_b_own = to_front(w_a, me), to_front(w_b, me)
        w_a_far, w_b_far = to_front(w_a, far), to_front(w_b, far)
        for i in range(pairs):
            far_out = []
            for h in range(2):
                b = 2 * i + h
                part[step, core, chip, b] = (
                    w_a_own[:, b : b + 1] * part[step, core, chip, b] + w_b_own[:, b : b + 1] * peer_part[step, chip, b]
                )
                far_out.append(
                    w_a_far[:, b : b + 1] * part[step, core, 1 - chip, b]
                    + w_b_far[:, b : b + 1] * peer_part[step, 1 - chip, b]
                )
            send_out[step, pl.ds(16 * i, 16), :] = jnp.concatenate(far_out, 0).astype(jnp.bfloat16)

    def merge_final(step):
        mine, theirs = own_lse[step], recv_lse[step]
        top = jnp.maximum(mine, theirs)
        w_a, w_b = jnp.exp2(mine - top), jnp.exp2(theirs - top)
        inverse = 1.0 / (w_a + w_b)
        w_a, w_b = w_a * inverse, w_b * inverse
        for i in range(pairs):
            other = recv_out[step, pl.ds(16 * i, 16), :].astype(jnp.float32)
            outs = []
            for h in range(2):
                b = 2 * i + h
                outs.append(
                    w_a[:, b : b + 1] * part[step, core, chip, b] + w_b[:, b : b + 1] * other[8 * h : 8 * h + 8]
                )
            out_buf[step, pl.ds(16 * i, 16), :] = jnp.concatenate(outs, 0).astype(jnp.bfloat16)

    def chip_stage(step):
        give_part(step).wait_recv()
        give_stat(step).wait_recv()
        merge_chip(step)
        give_out(step).start()
        give_lse(step).start()

    def final_stage(step):
        give_out(step).wait_recv()
        give_lse(step).wait_recv()
        merge_final(step)
        store_out(step).start()

    def attend(step, with_next):
        slot, at = lax.rem(step, RING), lax.rem(step, 2)
        next_slot, next_at = lax.rem(step + 1, RING), 1 - at
        peaks = jnp.zeros((ROWS, 128), jnp.float32)
        masses = jnp.zeros((ROWS, 128), jnp.float32)
        for i in range(pairs):
            if with_next:
                score_pair(step + 1, next_slot, next_at, i)
            peaks, masses = attend_pair(step, slot, at, i, peaks, masses)
        stat[step, 0] = peaks
        stat[step, 1] = masses

    last = num_chunks - 1
    for step in range(AHEAD):
        forward_q(step)
    await_q(0)
    load_k(0, 0).wait()
    for i in range(pairs):
        score_pair(0, 0, 0, i)
    load_k(RING, 0).start()

    @pl.loop(0, last)
    def _(step):
        @pl.when(step + AHEAD < num_chunks)
        def _():
            forward_q(step + AHEAD)

        await_q(step + 1)
        load_k(step + 1, lax.rem(step + 1, RING)).wait()
        load_v(step, lax.rem(step, RING)).wait()
        attend(step, True)

        @pl.when(step + 1 + RING < num_chunks)
        def _():
            load_k(step + 1 + RING, lax.rem(step + 1, RING)).start()

        @pl.when(step + RING < num_chunks)
        def _():
            load_v(step + RING, lax.rem(step, RING)).start()

        give_part(step).start()
        give_stat(step).start()

        @pl.when(step >= 2)
        def _():
            chip_stage(step - 2)

        @pl.when(step >= FINAL_LAG)
        def _():
            final_stage(step - FINAL_LAG)

    load_v(last, lax.rem(last, RING)).wait()
    attend(last, False)
    give_part(last).start()
    give_stat(last).start()

    @pl.loop(last - 2, num_chunks)
    def _(step):
        chip_stage(step)

    @pl.loop(last - FINAL_LAG, num_chunks)
    def _(step):
        final_stage(step)

    @pl.loop(0, num_chunks)
    def _(step):
        q_to_far(step, me).wait_send()
        q_to_sib(step, me).wait_send()
        q_forward(step, far).wait_send()
        give_part(step).wait_send()
        give_stat(step).wait_send()
        give_out(step).wait_send()
        give_lse(step).wait_send()
        store_out(step).wait()


def solution(mesh):
    def group_step(q_local, k_span, v_span, len_local):
        num_batch, span, dim = k_span.shape
        n = num_batch // CHUNK
        f32, bf16 = jnp.float32, jnp.bfloat16
        dma = lambda *shape: pltpu.SemaphoreType.DMA(shape)
        hbm = pl.BlockSpec(memory_space=pltpu.HBM)
        out = pl.pallas_call(
            functools.partial(kernel, n, dim**-0.5),
            out_shape=jax.ShapeDtypeStruct((num_batch * ROWS, dim), bf16),
            in_specs=[pl.BlockSpec(memory_space=pltpu.SMEM), hbm, hbm, hbm],
            out_specs=hbm,
            scratch_shapes=[
                pltpu.VMEM((RING, CHUNK, span, dim), bf16),
                pltpu.VMEM((RING, CHUNK, span, dim), bf16),
                pltpu.VMEM((num_batch, 4 * ROWS, dim), bf16),
                pltpu.VMEM((2, CHUNK // 2, 64, span), f32),
                pltpu.VMEM((n, 2, 2, CHUNK, ROWS, dim), f32),
                pltpu.VMEM((n, 2, ROWS, dim), f32),
                pltpu.VMEM((n, 2, CHUNK, ROWS, dim), f32),
                pltpu.VMEM((n, 2, ROWS, dim), f32),
                pltpu.VMEM((n, CHUNK * ROWS, dim), bf16),
                pltpu.VMEM((n, ROWS, dim), f32),
                pltpu.VMEM((n, CHUNK * ROWS, dim), bf16),
                pltpu.VMEM((n, ROWS, dim), f32),
                pltpu.VMEM((n, ROWS, dim), f32),
                pltpu.VMEM((n, CHUNK * ROWS, dim), bf16),
                dma(RING),
                dma(RING),
            ]
            + [dma(n)] * 16,
            compiler_params=pltpu.CompilerParams(
                collective_id=0, has_side_effects=True, vmem_limit_bytes=60 * 1024 * 1024
            ),
        )(len_local, q_local, k_span, v_span)
        return out.reshape(num_batch, ROWS, dim)

    return jax.shard_map(
        group_step,
        mesh=mesh,
        in_specs=(P("kv", "dup", None), P("kv", "dup", None), P("kv", "dup", None), P("kv")),
        out_specs=P("kv", "dup", None),
        check_vma=False,
    )
```

time: 130 us -> 70.4 us (0.54)
  Pallas kernels: 0 us -> 68.4 us
  waiting for transfers between devices: 49.2 us -> 0 us
  matrix products: 41.9 us -> 0 us
  other arithmetic: 16.3 us -> 0 us
  between operations: 13.5 us -> 0.01 us
  starting transfers between devices: 6.87 us -> 0 us
    pallas_call x0 -> x1, Pallas kernels: none -> 68.4 us  [group_step(): pl.pallas_call(functools.partial(kernel, n, dim ** (-0.5)), out_shape=jax...]
    dot_general x2 -> x0, matrix products: 41.9 us -> none  [the longest x1 23.4 us: group_step(): jnp.einsum('brd,bsd->brs', q_group, k_span, preferred_element_type=jnp.fl...]
    all_to_all x2 -> x0, waiting for transfers between devices: 25.1 us -> none  [the longest x1 25 us: group_step(): recv_out = lax.all_to_all(part_out, 'dup', 1, 1)]
    all_gather x1 -> x0, waiting for transfers between devices: 23.4 us -> none  [group_step(): q_group = lax.all_gather(q_local, 'dup', axis=1, tiled=True)]
    reduce_sum x3 -> x0, other arithmetic: 13.7 us -> none  [the longest x1 12.1 us: group_step(): row_mass = jnp.sum(prob_vals, axis=2, keepdims=True)]
    all_to_all x2 -> x0, starting transfers between devices: 6.87 us -> none  [the longest x1 3.61 us: group_step(): recv_out = lax.all_to_all(part_out, 'dup', 1, 1)]
    unnamed x0 -> x1, local copies, waits for them, and re-layouts: none -> 1.87 us
    reshape x1 -> x0, local copies, waits for them, and re-layouts: 1.71 us -> none  [group_step(): (weighted / row_mass).astype(jnp.bfloat16)]
  transfers between devices with their start and end apart: 3 -> 0, of which waited for: 2 -> 0; matrix products, arithmetic and copies ran while one was open for 16% -> 0% of each run, Pallas kernels for 0% -> 0%
where the time goes in v1:
time: 70.4 us; the launch traced here: 70.2 us
  Pallas kernels  68.4 us (97%)
  local copies, waits for them, and re-layouts  1.87 us (3%)
    pallas_call x1, Pallas kernels, group_step(): pl.pallas_call(functools.partial(kernel, n, dim ** (-0.5)), out_shape=jax...  68.4 us
    unnamed x1, local copies, waits for them, and re-layouts  1.87 us

profile of v1, /device:TPU:0, one launch (start us, length us, event | category | flops | bytes accessed | tf_op | source)
XLA Modules:
  0.0 70.2 jit_solution(3032870631150875273)
XLA Ops:
  0.0 68.4 %shard_map.46 = bf16[2048,128]{1,0:T(8,128)(2,1)} custom-call(s32[256]{0:T(256)} %len_ref.1, bf16[256,8,128]{2,1,0:T(8,128)(2,1)} %q_hbm.1, bf16[256,512,128]{2,1,0:T(8,128)(2,1)} %k_hbm.1, bf16[256,512,128]{2,1,0:T(8,128)(2,1)} %v_hbm.1), custom_call_target="tpu_custom_call" | custom-call | tf_op jit(solution)/shard_map/pallas_call | solution.py:319
  68.4 1.9 %copy.6 = bf16[256,8,128]{2,1,0:T(8,128)(2,1)} copy(bf16[256,8,128]{2,1,0:T(8,128)(2,1)} %bitcast.1) | data formatting | bytes 1048576

commit v2 on v1

--- a/solution.py
+++ b/solution.py
@@ -31,6 +31,7 @@
     vbuf,
     qbuf,
     sbuf,
+    pbuf,
     part,
     stat,
     peer_part,
@@ -144,29 +145,40 @@
     log2e = 1.0 / math.log(2.0)
     rate = scale * log2e
 
-    def score_pair(step, slot, at, i):
+    def score_pair(step, slot, i):
         b = step * CHUNK + 2 * i
         q_a, q_b = qbuf[b], qbuf[b + 1]
         none = jnp.zeros_like(q_a)
         left = jnp.concatenate([jnp.concatenate([q_a, none], 1), jnp.concatenate([none, q_b], 1)], 0)
         right = jnp.concatenate([kbuf[slot, 2 * i], kbuf[slot, 2 * i + 1]], 1)
-        sbuf[at, i] = lax.dot_general(left, right, (((1,), (1,)), ((), ())), preferred_element_type=jnp.float32)
-
-    def attend_pair(step, slot, at, i, peaks, masses):
-        probs = []
+        return lax.dot_general(left, right, (((1,), (1,)), ((), ())), preferred_element_type=jnp.float32)
+
+    def mask_pair(step, i, scores):
         for h in range(2):
             allowed = reach <= len_ref[step * CHUNK + 2 * i + h]
             for d in range(4):
-                s = sbuf[at, i, pl.ds(32 * h + 8 * d, 8), :]
-                s = jnp.where(allowed, s, LOWEST)
+                row = 32 * h + 8 * d
+                s = jnp.where(allowed, scores[row : row + 8], LOWEST)
+                sbuf[i, pl.ds(row, 8), :] = s
                 peak = jnp.maximum(jnp.max(s, axis=1, keepdims=True), FLOOR)
-                p = jnp.exp2((s - peak) * rate)
+                pbuf[i, pl.ds(row, 8), :] = jnp.broadcast_to(peak, (ROWS, 128))
+
+    def attend_pair(step, slot, i, peaks, masses):
+        probs = []
+        for h in range(2):
+            for d in range(4):
+                row = 32 * h + 8 * d
+                peak = pbuf[i, pl.ds(row, 8), :]
+                s = sbuf[i, pl.ds(row, 8), :]
+                p = jnp.exp2((s - jnp.concatenate([peak] * (span // 128), 1)) * rate)
                 mass = jnp.sum(p, axis=1, keepdims=True)
                 here = lane == (CHUNK * d + 2 * i + h)
                 peaks = jnp.where(here, peak, peaks)
                 masses = jnp.where(here, mass, masses)
                 probs.append(p)
-        p = jnp.concatenate(probs, 0).astype(jnp.bfloat16)
+        p = jnp.concatenate(
+            [jnp.concatenate(probs[j : j + 2], 0).astype(jnp.bfloat16) for j in range(0, 8, 2)], 0
+        )
         v = jnp.concatenate([vbuf[slot, 2 * i], vbuf[slot, 2 * i + 1]], 1)
         o = lax.dot_general(p, v, (((1,), (0,)), ((), ())), preferred_element_type=jnp.float32)
         for h in range(2):
@@ -234,14 +246,15 @@
         store_out(step).start()
 
     def attend(step, with_next):
-        slot, at = lax.rem(step, RING), lax.rem(step, 2)
-        next_slot, next_at = lax.rem(step + 1, RING), 1 - at
+        slot, next_slot = lax.rem(step, RING), lax.rem(step + 1, RING)
         peaks = jnp.zeros((ROWS, 128), jnp.float32)
         masses = jnp.zeros((ROWS, 128), jnp.float32)
         for i in range(pairs):
             if with_next:
-                score_pair(step + 1, next_slot, next_at, i)
-            peaks, masses = attend_pair(step, slot, at, i, peaks, masses)
+                scores = score_pair(step + 1, next_slot, i)
+            peaks, masses = attend_pair(step, slot, i, peaks, masses)
+            if with_next:
+                mask_pair(step + 1, i, scores)
         stat[step, 0] = peaks
         stat[step, 1] = masses
 
@@ -251,7 +264,7 @@
     await_q(0)
     load_k(0, 0).wait()
     for i in range(pairs):
-        score_pair(0, 0, 0, i)
+        mask_pair(0, i, score_pair(0, 0, i))
     load_k(RING, 0).start()
 
     @pl.loop(0, last)
@@ -325,7 +338,8 @@
                 pltpu.VMEM((RING, CHUNK, span, dim), bf16),
                 pltpu.VMEM((RING, CHUNK, span, dim), bf16),
                 pltpu.VMEM((num_batch, 4 * ROWS, dim), bf16),
-                pltpu.VMEM((2, CHUNK // 2, 64, span), f32),
+                pltpu.VMEM((CHUNK // 2, 64, span), f32),
+                pltpu.VMEM((CHUNK // 2, 64, 128), f32),
                 pltpu.VMEM((n, 2, 2, CHUNK, ROWS, dim), f32),
                 pltpu.VMEM((n, 2, ROWS, dim), f32),
                 pltpu.VMEM((n, 2, CHUNK, ROWS, dim), f32),

time: 70.4 us -> 44.8 us (0.64)
  Pallas kernels: 68.4 us -> 42.8 us
    pallas_call x1, Pallas kernels: 68.4 us -> 42.8 us  [group_step(): pl.pallas_call(functools.partial(kernel, n, dim ** (-0.5)), out_shape=jax...]
where the time goes in v2:
time: 44.8 us; the launch traced here: 44.7 us
  Pallas kernels  42.8 us (96%)
  local copies, waits for them, and re-layouts  1.87 us (4%)
    pallas_call x1, Pallas kernels, group_step(): pl.pallas_call(functools.partial(kernel, n, dim ** (-0.5)), out_shape=jax...  42.8 us
    unnamed x1, local copies, waits for them, and re-layouts  1.87 us

profile of v2, /device:TPU:0, one launch (start us, length us, event | category | flops | bytes accessed | tf_op | source)
XLA Modules:
  0.0 44.7 jit_solution(11099583243971969666)
XLA Ops:
  0.0 42.8 %shard_map.46 = bf16[2048,128]{1,0:T(8,128)(2,1)} custom-call(s32[256]{0:T(256)} %len_ref.1, bf16[256,8,128]{2,1,0:T(8,128)(2,1)} %q_hbm.1, bf16[256,512,128]{2,1,0:T(8,128)(2,1)} %k_hbm.1, bf16[256,512,128]{2,1,0:T(8,128)(2,1)} %v_hbm.1), custom_call_target="tpu_custom_call" | custom-call | tf_op jit(solution)/shard_map/pallas_call | solution.py:332
  42.8 1.9 %copy.6 = bf16[256,8,128]{2,1,0:T(8,128)(2,1)} copy(bf16[256,8,128]{2,1,0:T(8,128)(2,1)} %bitcast.1) | data formatting | bytes 1048576

commit v3 on v2

--- a/solution.py
+++ b/solution.py
@@ -12,8 +12,9 @@
 CHUNK = 16
 RING = 6
 AHEAD = 2
-FINAL_LAG = 10
+EARLY_FINALS = 8
 ROWS = 8
+OWN, FAR, SIB, FAR_SIB = range(4)
 MESH = pl.DeviceIdType.MESH
 LOWEST = -3.0e38
 FLOOR = -2.0e38
@@ -32,10 +33,12 @@
     qbuf,
     sbuf,
     pbuf,
-    part,
+    keep,
+    give,
+    peer,
     stat,
-    peer_part,
     peer_stat,
+    own_out,
     send_out,
     send_lse,
     recv_out,
@@ -65,9 +68,9 @@
     chip, core = me // 2, lax.rem(me, 2)
     sib = 2 * chip + (1 - core)
     far = 2 * (1 - chip) + core
-    far_sib = 2 * (1 - chip) + (1 - core)
     span = kbuf.shape[2]
     pairs = CHUNK // 2
+    n = num_chunks
 
     def load_k(step, slot):
         return pltpu.make_async_copy(k_hbm.at[pl.ds(step * CHUNK, CHUNK)], kbuf.at[slot], k_sem.at[slot])
@@ -75,31 +78,31 @@
     def load_v(step, slot):
         return pltpu.make_async_copy(v_hbm.at[pl.ds(step * CHUNK, CHUNK)], vbuf.at[slot], v_sem.at[slot])
 
-    def q_rows(step, owner):
-        return qbuf.at[pl.ds(step * CHUNK, CHUNK), pl.ds(pl.multiple_of(owner * ROWS, ROWS), ROWS)]
+    def q_rows(step, role):
+        return qbuf.at[pl.ds(step * CHUNK, CHUNK), pl.ds(role * ROWS, ROWS)]
 
     def q_mine(step):
         return q_hbm.at[pl.ds(step * CHUNK, CHUNK)]
 
     def keep_q(step):
-        return pltpu.make_async_copy(q_mine(step), q_rows(step, me), q_local.at[step])
+        return pltpu.make_async_copy(q_mine(step), q_rows(step, OWN), q_local.at[step])
 
     def remote(src, dst, send, recv, dev):
         return pltpu.make_async_remote_copy(
             src_ref=src, dst_ref=dst, send_sem=send, recv_sem=recv, device_id={"dup": dev}, device_id_type=MESH
         )
 
-    def q_to_far(step, owner):
-        return remote(q_mine(step), q_rows(step, owner), q_chip_send.at[step], q_chip_recv.at[step], far)
-
-    def q_to_sib(step, owner):
-        return remote(q_mine(step), q_rows(step, owner), q_sib_send.at[step], q_sib_recv.at[step], sib)
-
-    def q_forward(step, owner):
-        return remote(q_rows(step, owner), q_rows(step, owner), q_fwd_send.at[step], q_fwd_recv.at[step], sib)
+    def q_to_far(step):
+        return remote(q_mine(step), q_rows(step, FAR), q_chip_send.at[step], q_chip_recv.at[step], far)
+
+    def q_to_sib(step):
+        return remote(q_mine(step), q_rows(step, SIB), q_sib_send.at[step], q_sib_recv.at[step], sib)
+
+    def q_forward(step):
+        return remote(q_rows(step, FAR), q_rows(step, FAR_SIB), q_fwd_send.at[step], q_fwd_recv.at[step], sib)
 
     def give_part(step):
-        return remote(part.at[step, 1 - core], peer_part.at[step], part_send.at[step], part_recv.at[step], sib)
+        return remote(give.at[step], peer.at[step], part_send.at[step], part_recv.at[step], sib)
 
     def give_stat(step):
         return remote(stat.at[step], peer_stat.at[step], stat_send.at[step], stat_recv.at[step], sib)
@@ -124,26 +127,25 @@
         pl.semaphore_signal(barrier, inc=1, device_id={"dup": dev}, device_id_type=MESH)
     pl.semaphore_wait(barrier, 2)
 
-    @pl.loop(0, num_chunks)
-    def _(step):
-        q_to_far(step, me).start()
-        q_to_sib(step, me).start()
+    @pl.loop(0, n)
+    def _(step):
+        q_to_far(step).start()
+        q_to_sib(step).start()
         keep_q(step).start()
 
     def forward_q(step):
-        q_to_far(step, far).wait_recv()
-        q_forward(step, far).start()
+        q_to_far(step).wait_recv()
+        q_forward(step).start()
 
     def await_q(step):
         keep_q(step).wait()
-        q_to_sib(step, sib).wait_recv()
-        q_forward(step, far_sib).wait_recv()
+        q_to_sib(step).wait_recv()
+        q_forward(step).wait_recv()
 
     lane = lax.broadcasted_iota(jnp.int32, (ROWS, 128), 1)
     draft_of_row = lax.rem(lax.broadcasted_iota(jnp.int32, (ROWS, span), 0), DRAFT)
     reach = lax.broadcasted_iota(jnp.int32, (ROWS, span), 1) - draft_of_row + (me * span + DRAFT)
-    log2e = 1.0 / math.log(2.0)
-    rate = scale * log2e
+    rate = scale / math.log(2.0)
 
     def score_pair(step, slot, i):
         b = step * CHUNK + 2 * i
@@ -183,14 +185,13 @@
         o = lax.dot_general(p, v, (((1,), (0,)), ((), ())), preferred_element_type=jnp.float32)
         for h in range(2):
             for d in range(4):
-                part[step, d % 2, d // 2, 2 * i + h] = o[32 * h + 8 * d : 32 * h + 8 * d + 8, 128 * h : 128 * h + 128]
+                home = keep if d in (OWN, FAR) else give
+                home[step, d % 2, 2 * i + h] = o[32 * h + 8 * d : 32 * h + 8 * d + 8, 128 * h : 128 * h + 128]
         return peaks, masses
 
-    def to_front(tile, owner):
-        return pltpu.roll(tile, lax.rem(128 - owner * CHUNK, 128), 1)
-
     def merge_chip(step):
-        m_a, l_a, m_b, l_b = stat[step, 0], stat[step, 1], peer_stat[step, 0], peer_stat[step, 1]
+        m_a, l_a = stat[step, 0], stat[step, 1]
+        m_b, l_b = (pltpu.roll(peer_stat[step, j], 128 - SIB * CHUNK, 1) for j in range(2))
         top = jnp.maximum(m_a, m_b)
         w_a, w_b = jnp.exp2((m_a - top) * rate), jnp.exp2((m_b - top) * rate)
         total = w_a * l_a + w_b * l_b
@@ -199,21 +200,17 @@
         inverse = jnp.where(some, 1.0 / safe, 0.0)
         w_a, w_b = w_a * inverse, w_b * inverse
         lse = jnp.where(some, top * rate + jnp.log2(safe), LOWEST)
-        own_lse[step] = to_front(lse, me)
-        send_lse[step] = to_front(lse, far)
-        w_a_own, w_b_own = to_front(w_a, me), to_front(w_b, me)
-        w_a_far, w_b_far = to_front(w_a, far), to_front(w_b, far)
+        own_lse[step] = lse
+        send_lse[step] = pltpu.roll(lse, 128 - FAR * CHUNK, 1)
+
+        def both(role, b):
+            c = role * CHUNK + b
+            return w_a[:, c : c + 1] * keep[step, role, b] + w_b[:, c : c + 1] * peer[step, role, b]
+
         for i in range(pairs):
-            far_out = []
-            for h in range(2):
-                b = 2 * i + h
-                part[step, core, chip, b] = (
-                    w_a_own[:, b : b + 1] * part[step, core, chip, b] + w_b_own[:, b : b + 1] * peer_part[step, chip, b]
-                )
-                far_out.append(
-                    w_a_far[:, b : b + 1] * part[step, core, 1 - chip, b]
-                    + w_b_far[:, b : b + 1] * peer_part[step, 1 - chip, b]
-                )
+            for b in (2 * i, 2 * i + 1):
+                own_out[step, b] = both(OWN, b)
+            far_out = [both(FAR, b) for b in (2 * i, 2 * i + 1)]
             send_out[step, pl.ds(16 * i, 16), :] = jnp.concatenate(far_out, 0).astype(jnp.bfloat16)
 
     def merge_final(step):
@@ -227,15 +224,14 @@
             outs = []
             for h in range(2):
                 b = 2 * i + h
-                outs.append(
-                    w_a[:, b : b + 1] * part[step, core, chip, b] + w_b[:, b : b + 1] * other[8 * h : 8 * h + 8]
-                )
+                outs.append(w_a[:, b : b + 1] * own_out[step, b] + w_b[:, b : b + 1] * other[8 * h : 8 * h + 8])
             out_buf[step, pl.ds(16 * i, 16), :] = jnp.concatenate(outs, 0).astype(jnp.bfloat16)
 
-    def chip_stage(step):
+    def await_peer(step):
         give_part(step).wait_recv()
         give_stat(step).wait_recv()
-        merge_chip(step)
+
+    def send_far(step):
         give_out(step).start()
         give_lse(step).start()
 
@@ -258,7 +254,7 @@
         stat[step, 0] = peaks
         stat[step, 1] = masses
 
-    last = num_chunks - 1
+    last = n - 1
     for step in range(AHEAD):
         forward_q(step)
     await_q(0)
@@ -269,52 +265,65 @@
 
     @pl.loop(0, last)
     def _(step):
-        @pl.when(step + AHEAD < num_chunks)
+        @pl.when(step + AHEAD < n)
         def _():
             forward_q(step + AHEAD)
 
         await_q(step + 1)
         load_k(step + 1, lax.rem(step + 1, RING)).wait()
         load_v(step, lax.rem(step, RING)).wait()
+
+        @pl.when(step >= 2)
+        def _():
+            await_peer(step - 2)
+
+        ready = (step + n - 2) // n
+        merge_chip(ready * (step - 2) + (1 - ready) * n)
         attend(step, True)
 
-        @pl.when(step + 1 + RING < num_chunks)
+        @pl.when(step >= 2)
+        def _():
+            send_far(step - 2)
+
+        @pl.when(step + 1 + RING < n)
         def _():
             load_k(step + 1 + RING, lax.rem(step + 1, RING)).start()
 
-        @pl.when(step + RING < num_chunks)
+        @pl.when(step + RING < n)
         def _():
             load_v(step + RING, lax.rem(step, RING)).start()
 
         give_part(step).start()
         give_stat(step).start()
 
-        @pl.when(step >= 2)
-        def _():
-            chip_stage(step - 2)
-
-        @pl.when(step >= FINAL_LAG)
-        def _():
-            final_stage(step - FINAL_LAG)
-
     load_v(last, lax.rem(last, RING)).wait()
+    await_peer(last - 2)
+    merge_chip(last - 2)
     attend(last, False)
+    send_far(last - 2)
     give_part(last).start()
     give_stat(last).start()
-
-    @pl.loop(last - 2, num_chunks)
-    def _(step):
-        chip_stage(step)
-
-    @pl.loop(last - FINAL_LAG, num_chunks)
+    await_peer(last - 1)
+    merge_chip(last - 1)
+    send_far(last - 1)
+
+    @pl.loop(0, EARLY_FINALS)
     def _(step):
         final_stage(step)
 
-    @pl.loop(0, num_chunks)
-    def _(step):
-        q_to_far(step, me).wait_send()
-        q_to_sib(step, me).wait_send()
-        q_forward(step, far).wait_send()
+    await_peer(last)
+    merge_chip(last)
+    send_far(last)
+
+    @pl.loop(EARLY_FINALS, n)
+    def _(step):
+        final_stage(step)
+
+    @pl.loop(0, n)
+    def _(step):
+        q_to_far(step).wait_send()
+        q_to_sib(step).wait_send()
+        q_forward(step).wait_send()
         give_part(step).wait_send()
         give_stat(step).wait_send()
         give_out(step).wait_send()
@@ -340,15 +349,17 @@
                 pltpu.VMEM((num_batch, 4 * ROWS, dim), bf16),
                 pltpu.VMEM((CHUNK // 2, 64, span), f32),
                 pltpu.VMEM((CHUNK // 2, 64, 128), f32),
-                pltpu.VMEM((n, 2, 2, CHUNK, ROWS, dim), f32),
-                pltpu.VMEM((n, 2, ROWS, dim), f32),
+                pltpu.VMEM((n + 1, 2, CHUNK, ROWS, dim), f32),
                 pltpu.VMEM((n, 2, CHUNK, ROWS, dim), f32),
-                pltpu.VMEM((n, 2, ROWS, dim), f32),
+                pltpu.VMEM((n + 1, 2, CHUNK, ROWS, dim), f32),
+                pltpu.VMEM((n + 1, 2, ROWS, dim), f32),
+                pltpu.VMEM((n + 1, 2, ROWS, dim), f32),
+                pltpu.VMEM((n + 1, CHUNK, ROWS, dim), f32),
+                pltpu.VMEM((n + 1, CHUNK * ROWS, dim), bf16),
+                pltpu.VMEM((n + 1, ROWS, dim), f32),
                 pltpu.VMEM((n, CHUNK * ROWS, dim), bf16),
                 pltpu.VMEM((n, ROWS, dim), f32),
-                pltpu.VMEM((n, CHUNK * ROWS, dim), bf16),
-                pltpu.VMEM((n, ROWS, dim), f32),
-                pltpu.VMEM((n, ROWS, dim), f32),
+                pltpu.VMEM((n + 1, ROWS, dim), f32),
                 pltpu.VMEM((n, CHUNK * ROWS, dim), bf16),
                 dma(RING),
                 dma(RING),

time: 44.8 us -> 40.9 us (0.913)
  Pallas kernels: 42.8 us -> 38.9 us
    pallas_call x1, Pallas kernels: 42.8 us -> 38.9 us  [group_step(): pl.pallas_call(functools.partial(kernel, n, dim ** (-0.5)), out_shape=jax...]
where the time goes in v3:
time: 40.9 us; the launch traced here: 40.8 us
  Pallas kernels  38.9 us (95%)
  local copies, waits for them, and re-layouts  1.87 us (5%)
    pallas_call x1, Pallas kernels, group_step(): pl.pallas_call(functools.partial(kernel, n, dim ** (-0.5)), out_shape=jax...  38.9 us
    unnamed x1, local copies, waits for them, and re-layouts  1.87 us

profile of v3, /device:TPU:0, one launch (start us, length us, event | category | flops | bytes accessed | tf_op | source)
XLA Modules:
  0.0 40.8 jit_solution(15857394210911150133)
XLA Ops:
  0.0 38.9 %shard_map.46 = bf16[2048,128]{1,0:T(8,128)(2,1)} custom-call(s32[256]{0:T(256)} %len_ref.1, bf16[256,8,128]{2,1,0:T(8,128)(2,1)} %q_hbm.1, bf16[256,512,128]{2,1,0:T(8,128)(2,1)} %k_hbm.1, bf16[256,512,128]{2,1,0:T(8,128)(2,1)} %v_hbm.1), custom_call_target="tpu_custom_call" | custom-call | tf_op jit(solution)/shard_map/pallas_call | solution.py:341
  38.9 1.9 %copy.6 = bf16[256,8,128]{2,1,0:T(8,128)(2,1)} copy(bf16[256,8,128]{2,1,0:T(8,128)(2,1)} %bitcast.1) | data formatting | bytes 1048576

commit v4 on v3

--- a/solution.py
+++ b/solution.py
@@ -79,10 +79,10 @@
         return pltpu.make_async_copy(v_hbm.at[pl.ds(step * CHUNK, CHUNK)], vbuf.at[slot], v_sem.at[slot])
 
     def q_rows(step, role):
-        return qbuf.at[pl.ds(step * CHUNK, CHUNK), pl.ds(role * ROWS, ROWS)]
+        return qbuf.at[role, pl.ds(step * CHUNK * ROWS, CHUNK * ROWS)]
 
     def q_mine(step):
-        return q_hbm.at[pl.ds(step * CHUNK, CHUNK)]
+        return q_hbm.at[pl.ds(step * CHUNK * ROWS, CHUNK * ROWS)]
 
     def keep_q(step):
         return pltpu.make_async_copy(q_mine(step), q_rows(step, OWN), q_local.at[step])
@@ -147,11 +147,14 @@
     reach = lax.broadcasted_iota(jnp.int32, (ROWS, span), 1) - draft_of_row + (me * span + DRAFT)
     rate = scale / math.log(2.0)
 
+    first = lax.rem(lax.broadcasted_iota(jnp.int32, (16, 128), 0), 16) < ROWS
+    of_first = jnp.where(first, 1.0, 0.0).astype(jnp.bfloat16)
+    of_second = jnp.where(first, 0.0, 1.0).astype(jnp.bfloat16)
+
     def score_pair(step, slot, i):
-        b = step * CHUNK + 2 * i
-        q_a, q_b = qbuf[b], qbuf[b + 1]
-        none = jnp.zeros_like(q_a)
-        left = jnp.concatenate([jnp.concatenate([q_a, none], 1), jnp.concatenate([none, q_b], 1)], 0)
+        start = pl.multiple_of(step * CHUNK * ROWS, 16) + 16 * i
+        q = [qbuf[role, pl.ds(start, 16), :] for role in range(4)]
+        left = jnp.concatenate([jnp.concatenate([x * of_first, x * of_second], 1) for x in q], 0)
         right = jnp.concatenate([kbuf[slot, 2 * i], kbuf[slot, 2 * i + 1]], 1)
         return lax.dot_general(left, right, (((1,), (1,)), ((), ())), preferred_element_type=jnp.float32)
 
@@ -159,7 +162,7 @@
         for h in range(2):
             allowed = reach <= len_ref[step * CHUNK + 2 * i + h]
             for d in range(4):
-                row = 32 * h + 8 * d
+                row = 16 * d + 8 * h
                 s = jnp.where(allowed, scores[row : row + 8], LOWEST)
                 sbuf[i, pl.ds(row, 8), :] = s
                 peak = jnp.maximum(jnp.max(s, axis=1, keepdims=True), FLOOR)
@@ -167,9 +170,9 @@
 
     def attend_pair(step, slot, i, peaks, masses):
         probs = []
-        for h in range(2):
-            for d in range(4):
-                row = 32 * h + 8 * d
+        for d in range(4):
+            for h in range(2):
+                row = 16 * d + 8 * h
                 peak = pbuf[i, pl.ds(row, 8), :]
                 s = sbuf[i, pl.ds(row, 8), :]
                 p = jnp.exp2((s - jnp.concatenate([peak] * (span // 128), 1)) * rate)
@@ -186,7 +189,7 @@
         for h in range(2):
             for d in range(4):
                 home = keep if d in (OWN, FAR) else give
-                home[step, d % 2, 2 * i + h] = o[32 * h + 8 * d : 32 * h + 8 * d + 8, 128 * h : 128 * h + 128]
+                home[step, d % 2, 2 * i + h] = o[16 * d + 8 * h : 16 * d + 8 * h + 8, 128 * h : 128 * h + 128]
         return peaks, masses
 
     def merge_chip(step):
@@ -346,7 +349,7 @@
             scratch_shapes=[
                 pltpu.VMEM((RING, CHUNK, span, dim), bf16),
                 pltpu.VMEM((RING, CHUNK, span, dim), bf16),
-                pltpu.VMEM((num_batch, 4 * ROWS, dim), bf16),
+                pltpu.VMEM((4, num_batch * ROWS, dim), bf16),
                 pltpu.VMEM((CHUNK // 2, 64, span), f32),
                 pltpu.VMEM((CHUNK // 2, 64, 128), f32),
                 pltpu.VMEM((n + 1, 2, CHUNK, ROWS, dim), f32),
@@ -368,7 +371,7 @@
             compiler_params=pltpu.CompilerParams(
                 collective_id=0, has_side_effects=True, vmem_limit_bytes=60 * 1024 * 1024
             ),
-        )(len_local, q_local, k_span, v_span)
+        )(len_local, q_local.reshape(num_batch * ROWS, dim), k_span, v_span)
         return out.reshape(num_batch, ROWS, dim)
 
     return jax.shard_map(

time: 40.9 us -> 41 us (level)
  no operation moved by 1% of the time
where the time goes in v4:
time: 41 us; the launch traced here: 40.9 us
  Pallas kernels  39 us (95%)
  local copies, waits for them, and re-layouts  1.87 us (5%)
    pallas_call x1, Pallas kernels, group_step(): pl.pallas_call(functools.partial(kernel, n, dim ** (-0.5)), out_shape=jax...  39 us
    unnamed x1, local copies, waits for them, and re-layouts  1.87 us

profile of v4, /device:TPU:0, one launch (start us, length us, event | category | flops | bytes accessed | tf_op | source)
XLA Modules:
  0.0 40.9 jit_solution(12061087500109722219)
XLA Ops:
  0.0 39.0 %shard_map.46 = bf16[2048,128]{1,0:T(8,128)(2,1)} custom-call(s32[256]{0:T(256)} %len_ref.1, bf16[2048,128]{1,0:T(8,128)(2,1)} %bitcast.3, bf16[256,512,128]{2,1,0:T(8,128)(2,1)} %k_hbm.1, bf16[256,512,128]{2,1,0:T(8,128)(2,1)} %v_hbm.1), custom_call_target="tpu_custom_call" | custom-call | tf_op jit(solution)/shard_map/pallas_call | solution.py:344
  39.0 1.9 %copy.6 = bf16[256,8,128]{2,1,0:T(8,128)(2,1)} copy(bf16[256,8,128]{2,1,0:T(8,128)(2,1)} %bitcast.2) | data formatting | bytes 1048576

commit v5 on v4

--- a/solution.py
+++ b/solution.py
@@ -82,10 +82,7 @@
         return qbuf.at[role, pl.ds(step * CHUNK * ROWS, CHUNK * ROWS)]
 
     def q_mine(step):
-        return q_hbm.at[pl.ds(step * CHUNK * ROWS, CHUNK * ROWS)]
-
-    def keep_q(step):
-        return pltpu.make_async_copy(q_mine(step), q_rows(step, OWN), q_local.at[step])
+        return q_rows(step, OWN)
 
     def remote(src, dst, send, recv, dev):
         return pltpu.make_async_remote_copy(
@@ -118,6 +115,8 @@
             out_buf.at[step], out_hbm.at[pl.ds(step * CHUNK * ROWS, CHUNK * ROWS)], out_sem.at[step]
         )
 
+    whole_q = pltpu.make_async_copy(q_hbm, qbuf.at[OWN], q_local.at[0])
+    whole_q.start()
     for step in range(RING):
         load_k(step, step).start()
         load_v(step, step).start()
@@ -126,19 +125,19 @@
     for dev in (sib, far):
         pl.semaphore_signal(barrier, inc=1, device_id={"dup": dev}, device_id_type=MESH)
     pl.semaphore_wait(barrier, 2)
+    whole_q.wait()
+    q_to_far(0).start()
+    q_to_far(1).start()
 
     @pl.loop(0, n)
     def _(step):
-        q_to_far(step).start()
         q_to_sib(step).start()
-        keep_q(step).start()
 
     def forward_q(step):
         q_to_far(step).wait_recv()
         q_forward(step).start()
 
     def await_q(step):
-        keep_q(step).wait()
         q_to_sib(step).wait_recv()
         q_forward(step).wait_recv()
 
@@ -258,8 +257,11 @@
         stat[step, 1] = masses
 
     last = n - 1
-    for step in range(AHEAD):
-        forward_q(step)
+    forward_q(0)
+    q_to_far(2).start()
+    forward_q(1)
+    q_to_far(3).start()
+    q_to_far(4).start()
     await_q(0)
     load_k(0, 0).wait()
     for i in range(pairs):
@@ -268,6 +270,10 @@
 
     @pl.loop(0, last)
     def _(step):
+        @pl.when(step + 5 < n)
+        def _():
+            q_to_far(step + 5).start()
+
         @pl.when(step + AHEAD < n)
         def _():
             forward_q(step + AHEAD)
@@ -366,8 +372,9 @@
                 pltpu.VMEM((n, CHUNK * ROWS, dim), bf16),
                 dma(RING),
                 dma(RING),
+                dma(1),
             ]
-            + [dma(n)] * 16,
+            + [dma(n)] * 15,
             compiler_params=pltpu.CompilerParams(
                 collective_id=0, has_side_effects=True, vmem_limit_bytes=60 * 1024 * 1024
             ),

time: 41 us -> 45.9 us (1.12)
  Pallas kernels: 39 us -> 43.9 us
    pallas_call x1, Pallas kernels: 39 us -> 43.9 us  [group_step(): pl.pallas_call(functools.partial(kernel, n, dim ** (-0.5)), out_shape=jax...]
where the time goes in v5:
time: 45.9 us; the launch traced here: 45.8 us
  Pallas kernels  43.9 us (96%)
  local copies, waits for them, and re-layouts  1.87 us (4%)
    pallas_call x1, Pallas kernels, group_step(): pl.pallas_call(functools.partial(kernel, n, dim ** (-0.5)), out_shape=jax...  43.9 us
    unnamed x1, local copies, waits for them, and re-layouts  1.87 us

profile of v5, /device:TPU:0, one launch (start us, length us, event | category | flops | bytes accessed | tf_op | source)
XLA Modules:
  0.0 45.8 jit_solution(3171101559350335810)
XLA Ops:
  0.0 43.9 %shard_map.46 = bf16[2048,128]{1,0:T(8,128)(2,1)} custom-call(s32[256]{0:T(256)} %len_ref.1, bf16[2048,128]{1,0:T(8,128)(2,1)} %bitcast.3, bf16[256,512,128]{2,1,0:T(8,128)(2,1)} %k_hbm.1, bf16[256,512,128]{2,1,0:T(8,128)(2,1)} %v_hbm.1), custom_call_target="tpu_custom_call" | custom-call | tf_op jit(solution)/shard_map/pallas_call | solution.py:350
  43.9 1.9 %copy.6 = bf16[256,8,128]{2,1,0:T(8,128)(2,1)} copy(bf16[256,8,128]{2,1,0:T(8,128)(2,1)} %bitcast.2) | data formatting | bytes 1048576

commit v6 on v5

--- a/solution.py
+++ b/solution.py
@@ -10,7 +10,7 @@
 
 DRAFT = 4
 CHUNK = 16
-RING = 6
+RING = 3
 AHEAD = 2
 EARLY_FINALS = 8
 ROWS = 8

time: 45.9 us -> 42.3 us (0.922)
  Pallas kernels: 43.9 us -> 40.3 us
    pallas_call x1, Pallas kernels: 43.9 us -> 40.3 us  [group_step(): pl.pallas_call(functools.partial(kernel, n, dim ** (-0.5)), out_shape=jax...]
where the time goes in v6:
time: 42.3 us; the launch traced here: 42.2 us
  Pallas kernels  40.3 us (95%)
  local copies, waits for them, and re-layouts  1.87 us (4%)
    pallas_call x1, Pallas kernels, group_step(): pl.pallas_call(functools.partial(kernel, n, dim ** (-0.5)), out_shape=jax...  40.3 us
    unnamed x1, local copies, waits for them, and re-layouts  1.87 us

profile of v6, /device:TPU:0, one launch (start us, length us, event | category | flops | bytes accessed | tf_op | source)
XLA Modules:
  0.0 42.2 jit_solution(7523219946323004517)
XLA Ops:
  0.0 40.3 %shard_map.46 = bf16[2048,128]{1,0:T(8,128)(2,1)} custom-call(s32[256]{0:T(256)} %len_ref.1, bf16[2048,128]{1,0:T(8,128)(2,1)} %bitcast.3, bf16[256,512,128]{2,1,0:T(8,128)(2,1)} %k_hbm.1, bf16[256,512,128]{2,1,0:T(8,128)(2,1)} %v_hbm.1), custom_call_target="tpu_custom_call" | custom-call | tf_op jit(solution)/shard_map/pallas_call | solution.py:350
  40.3 1.9 %copy.6 = bf16[256,8,128]{2,1,0:T(8,128)(2,1)} copy(bf16[256,8,128]{2,1,0:T(8,128)(2,1)} %bitcast.2) | data formatting | bytes 1048576

commit v7 on v5

--- a/solution.py
+++ b/solution.py
@@ -117,21 +117,24 @@
 
     whole_q = pltpu.make_async_copy(q_hbm, qbuf.at[OWN], q_local.at[0])
     whole_q.start()
-    for step in range(RING):
-        load_k(step, step).start()
-        load_v(step, step).start()
+    load_k(0, 0).start()
 
     barrier = pltpu.get_barrier_semaphore()
     for dev in (sib, far):
         pl.semaphore_signal(barrier, inc=1, device_id={"dup": dev}, device_id_type=MESH)
     pl.semaphore_wait(barrier, 2)
     whole_q.wait()
-    q_to_far(0).start()
-    q_to_far(1).start()
+    for step in range(4):
+        q_to_far(step).start()
 
     @pl.loop(0, n)
     def _(step):
         q_to_sib(step).start()
+
+    load_v(0, 0).start()
+    for step in range(1, RING):
+        load_k(step, step).start()
+        load_v(step, step).start()
 
     def forward_q(step):
         q_to_far(step).wait_recv()
@@ -257,11 +260,10 @@
         stat[step, 1] = masses
 
     last = n - 1
-    forward_q(0)
-    q_to_far(2).start()
-    forward_q(1)
-    q_to_far(3).start()
-    q_to_far(4).start()
+    for step in range(AHEAD):
+        forward_q(step)
+        q_to_far(2 * step + 4).start()
+        q_to_far(2 * step + 5).start()
     await_q(0)
     load_k(0, 0).wait()
     for i in range(pairs):
@@ -270,9 +272,10 @@
 
     @pl.loop(0, last)
     def _(step):
-        @pl.when(step + 5 < n)
-        def _():
-            q_to_far(step + 5).start()
+        @pl.when(2 * step + 2 * AHEAD + 4 < n)
+        def _():
+            q_to_far(2 * step + 2 * AHEAD + 4).start()
+            q_to_far(2 * step + 2 * AHEAD + 5).start()
 
         @pl.when(step + AHEAD < n)
         def _():

time: 45.9 us -> 38.1 us (0.83)
  Pallas kernels: 43.9 us -> 36.1 us
    pallas_call x1, Pallas kernels: 43.9 us -> 36.1 us  [group_step(): pl.pallas_call(functools.partial(kernel, n, dim ** (-0.5)), out_shape=jax...]
where the time goes in v7:
time: 38.1 us; the launch traced here: 38 us
  Pallas kernels  36.1 us (95%)
  local copies, waits for them, and re-layouts  1.87 us (5%)
    pallas_call x1, Pallas kernels, group_step(): pl.pallas_call(functools.partial(kernel, n, dim ** (-0.5)), out_shape=jax...  36.1 us
    unnamed x1, local copies, waits for them, and re-layouts  1.87 us

profile of v7, /device:TPU:0, one launch (start us, length us, event | category | flops | bytes accessed | tf_op | source)
XLA Modules:
  0.0 38.0 jit_solution(10632391005655217003)
XLA Ops:
  0.0 36.1 %shard_map.46 = bf16[2048,128]{1,0:T(8,128)(2,1)} custom-call(s32[256]{0:T(256)} %len_ref.1, bf16[2048,128]{1,0:T(8,128)(2,1)} %bitcast.3, bf16[256,512,128]{2,1,0:T(8,128)(2,1)} %k_hbm.1, bf16[256,512,128]{2,1,0:T(8,128)(2,1)} %v_hbm.1), custom_call_target="tpu_custom_call" | custom-call | tf_op jit(solution)/shard_map/pallas_call | solution.py:353
  36.1 1.9 %copy.6 = bf16[256,8,128]{2,1,0:T(8,128)(2,1)} copy(bf16[256,8,128]{2,1,0:T(8,128)(2,1)} %bitcast.2) | data formatting | bytes 1048576

commit v8 on v7

--- a/solution.py
+++ b/solution.py
@@ -10,8 +10,8 @@
 
 DRAFT = 4
 CHUNK = 16
-RING = 6
-AHEAD = 2
+RING = 2
+AHEAD = 3
 EARLY_FINALS = 8
 ROWS = 8
 OWN, FAR, SIB, FAR_SIB = range(4)

time: 38.1 us -> 45.5 us (1.19)
  Pallas kernels: 36.1 us -> 43.4 us
    pallas_call x1, Pallas kernels: 36.1 us -> 43.4 us  [group_step(): pl.pallas_call(functools.partial(kernel, n, dim ** (-0.5)), out_shape=jax...]
where the time goes in v8:
time: 45.5 us; the launch traced here: 45.3 us
  Pallas kernels  43.4 us (95%)
  local copies, waits for them, and re-layouts  1.87 us (4%)
    pallas_call x1, Pallas kernels, group_step(): pl.pallas_call(functools.partial(kernel, n, dim ** (-0.5)), out_shape=jax...  43.4 us
    unnamed x1, local copies, waits for them, and re-layouts  1.87 us

profile of v8, /device:TPU:0, one launch (start us, length us, event | category | flops | bytes accessed | tf_op | source)
XLA Modules:
  0.0 45.3 jit_solution(789832833070110708)
XLA Ops:
  0.0 43.4 %shard_map.46 = bf16[2048,128]{1,0:T(8,128)(2,1)} custom-call(s32[256]{0:T(256)} %len_ref.1, bf16[2048,128]{1,0:T(8,128)(2,1)} %bitcast.3, bf16[256,512,128]{2,1,0:T(8,128)(2,1)} %k_hbm.1, bf16[256,512,128]{2,1,0:T(8,128)(2,1)} %v_hbm.1), custom_call_target="tpu_custom_call" | custom-call | tf_op jit(solution)/shard_map/pallas_call | solution.py:353
  43.4 1.9 %copy.6 = bf16[256,8,128]{2,1,0:T(8,128)(2,1)} copy(bf16[256,8,128]{2,1,0:T(8,128)(2,1)} %bitcast.2) | data formatting | bytes 1048576

commit v9 on v7

--- a/solution.py
+++ b/solution.py
@@ -12,6 +12,7 @@
 CHUNK = 16
 RING = 6
 AHEAD = 2
+LAG = 3
 EARLY_FINALS = 8
 ROWS = 8
 OWN, FAR, SIB, FAR_SIB = range(4)
@@ -285,39 +286,41 @@
         load_k(step + 1, lax.rem(step + 1, RING)).wait()
         load_v(step, lax.rem(step, RING)).wait()
 
-        @pl.when(step >= 2)
-        def _():
-            await_peer(step - 2)
-
-        ready = (step + n - 2) // n
-        merge_chip(ready * (step - 2) + (1 - ready) * n)
+        @pl.when(step >= LAG)
+        def _():
+            await_peer(step - LAG)
+
+        ready = (step + n - LAG) // n
+        merge_chip(ready * (step - LAG) + (1 - ready) * n)
         attend(step, True)
-
-        @pl.when(step >= 2)
-        def _():
-            send_far(step - 2)
-
-        @pl.when(step + 1 + RING < n)
-        def _():
-            load_k(step + 1 + RING, lax.rem(step + 1, RING)).start()
-
-        @pl.when(step + RING < n)
-        def _():
-            load_v(step + RING, lax.rem(step, RING)).start()
-
         give_part(step).start()
         give_stat(step).start()
 
+        @pl.when(step >= LAG)
+        def _():
+            send_far(step - LAG)
+
+        @pl.when(step + 1 + RING < n)
+        def _():
+            load_k(step + 1 + RING, lax.rem(step + 1, RING)).start()
+
+        @pl.when(step + RING < n)
+        def _():
+            load_v(step + RING, lax.rem(step, RING)).start()
+
     load_v(last, lax.rem(last, RING)).wait()
-    await_peer(last - 2)
-    merge_chip(last - 2)
+    await_peer(last - LAG)
+    merge_chip(last - LAG)
     attend(last, False)
-    send_far(last - 2)
     give_part(last).start()
     give_stat(last).start()
-    await_peer(last - 1)
-    merge_chip(last - 1)
-    send_far(last - 1)
+    send_far(last - LAG)
+
+    @pl.loop(last - LAG + 1, last)
+    def _(step):
+        await_peer(step)
+        merge_chip(step)
+        send_far(step)
 
     @pl.loop(0, EARLY_FINALS)
     def _(step):

time: 38.1 us -> 38.5 us (1.010)
  Pallas kernels: 36.1 us -> 36.5 us
where the time goes in v9:
time: 38.5 us; the launch traced here: 38.3 us
  Pallas kernels  36.5 us (95%)
  local copies, waits for them, and re-layouts  1.87 us (5%)
    pallas_call x1, Pallas kernels, group_step(): pl.pallas_call(functools.partial(kernel, n, dim ** (-0.5)), out_shape=jax...  36.5 us
    unnamed x1, local copies, waits for them, and re-layouts  1.87 us

profile of v9, /device:TPU:0, one launch (start us, length us, event | category | flops | bytes accessed | tf_op | source)
XLA Modules:
  0.0 38.3 jit_solution(15890217510617921523)
XLA Ops:
  0.0 36.5 %shard_map.46 = bf16[2048,128]{1,0:T(8,128)(2,1)} custom-call(s32[256]{0:T(256)} %len_ref.1, bf16[2048,128]{1,0:T(8,128)(2,1)} %bitcast.3, bf16[256,512,128]{2,1,0:T(8,128)(2,1)} %k_hbm.1, bf16[256,512,128]{2,1,0:T(8,128)(2,1)} %v_hbm.1), custom_call_target="tpu_custom_call" | custom-call | tf_op jit(solution)/shard_map/pallas_call | solution.py:356
  36.5 1.9 %copy.6 = bf16[256,8,128]{2,1,0:T(8,128)(2,1)} copy(bf16[256,8,128]{2,1,0:T(8,128)(2,1)} %bitcast.2) | data formatting | bytes 1048576

commit v10 on v9

--- a/solution.py
+++ b/solution.py
@@ -12,8 +12,10 @@
 CHUNK = 16
 RING = 6
 AHEAD = 2
-LAG = 3
-EARLY_FINALS = 8
+LAG = 2
+FINAL_LAG = 8
+EARLY_FINALS = 4
+PV_LAG = 2
 ROWS = 8
 OWN, FAR, SIB, FAR_SIB = range(4)
 MESH = pl.DeviceIdType.MESH
@@ -34,6 +36,7 @@
     qbuf,
     sbuf,
     pbuf,
+    ebuf,
     keep,
     give,
     peer,
@@ -171,9 +174,9 @@
                 peak = jnp.maximum(jnp.max(s, axis=1, keepdims=True), FLOOR)
                 pbuf[i, pl.ds(row, 8), :] = jnp.broadcast_to(peak, (ROWS, 128))
 
-    def attend_pair(step, slot, i, peaks, masses):
-        probs = []
+    def weigh_pair(i, peaks, masses):
         for d in range(4):
+            probs = []
             for h in range(2):
                 row = 16 * d + 8 * h
                 peak = pbuf[i, pl.ds(row, 8), :]
@@ -184,16 +187,16 @@
                 peaks = jnp.where(here, peak, peaks)
                 masses = jnp.where(here, mass, masses)
                 probs.append(p)
-        p = jnp.concatenate(
-            [jnp.concatenate(probs[j : j + 2], 0).astype(jnp.bfloat16) for j in range(0, 8, 2)], 0
-        )
+            ebuf[i, pl.ds(16 * d, 16), :] = jnp.concatenate(probs, 0).astype(jnp.bfloat16)
+        return peaks, masses
+
+    def sum_pair(step, slot, i):
         v = jnp.concatenate([vbuf[slot, 2 * i], vbuf[slot, 2 * i + 1]], 1)
-        o = lax.dot_general(p, v, (((1,), (0,)), ((), ())), preferred_element_type=jnp.float32)
+        o = lax.dot_general(ebuf[i], v, (((1,), (0,)), ((), ())), preferred_element_type=jnp.float32)
         for h in range(2):
             for d in range(4):
                 home = keep if d in (OWN, FAR) else give
                 home[step, d % 2, 2 * i + h] = o[16 * d + 8 * h : 16 * d + 8 * h + 8, 128 * h : 128 * h + 128]
-        return peaks, masses
 
     def merge_chip(step):
         m_a, l_a = stat[step, 0], stat[step, 1]
@@ -241,9 +244,12 @@
         give_out(step).start()
         give_lse(step).start()
 
-    def final_stage(step):
+    def await_far(step):
         give_out(step).wait_recv()
         give_lse(step).wait_recv()
+
+    def final_stage(step):
+        await_far(step)
         merge_final(step)
         store_out(step).start()
 
@@ -251,12 +257,16 @@
         slot, next_slot = lax.rem(step, RING), lax.rem(step + 1, RING)
         peaks = jnp.zeros((ROWS, 128), jnp.float32)
         masses = jnp.zeros((ROWS, 128), jnp.float32)
-        for i in range(pairs):
-            if with_next:
-                scores = score_pair(step + 1, next_slot, i)
-            peaks, masses = attend_pair(step, slot, i, peaks, masses)
-            if with_next:
-                mask_pair(step + 1, i, scores)
+        scores = [None] * pairs
+        for i in range(pairs + PV_LAG):
+            if i < pairs:
+                peaks, masses = weigh_pair(i, peaks, masses)
+                if with_next:
+                    scores[i] = score_pair(step + 1, next_slot, i)
+            if i >= PV_LAG:
+                sum_pair(step, slot, i - PV_LAG)
+            if with_next and 1 <= i <= pairs:
+                mask_pair(step + 1, i - 1, scores[i - 1])
         stat[step, 0] = peaks
         stat[step, 1] = masses
 
@@ -290,6 +300,12 @@
         def _():
             await_peer(step - LAG)
 
+        @pl.when(step >= FINAL_LAG)
+        def _():
+            await_far(step - FINAL_LAG)
+
+        done = (step + n - FINAL_LAG) // n
+        merge_final(done * (step - FINAL_LAG) + (1 - done) * n)
         ready = (step + n - LAG) // n
         merge_chip(ready * (step - LAG) + (1 - ready) * n)
         attend(step, True)
@@ -300,6 +316,10 @@
         def _():
             send_far(step - LAG)
 
+        @pl.when(step >= FINAL_LAG)
+        def _():
+            store_out(step - FINAL_LAG).start()
+
         @pl.when(step + 1 + RING < n)
         def _():
             load_k(step + 1 + RING, lax.rem(step + 1, RING)).start()
@@ -310,8 +330,11 @@
 
     load_v(last, lax.rem(last, RING)).wait()
     await_peer(last - LAG)
+    await_far(last - FINAL_LAG)
+    merge_final(last - FINAL_LAG)
     merge_chip(last - LAG)
     attend(last, False)
+    store_out(last - FINAL_LAG).start()
     give_part(last).start()
     give_stat(last).start()
     send_far(last - LAG)
@@ -322,7 +345,7 @@
         merge_chip(step)
         send_far(step)
 
-    @pl.loop(0, EARLY_FINALS)
+    @pl.loop(last - FINAL_LAG + 1, last - FINAL_LAG + 1 + EARLY_FINALS)
     def _(step):
         final_stage(step)
 
@@ -330,7 +353,7 @@
     merge_chip(last)
     send_far(last)
 
-    @pl.loop(EARLY_FINALS, n)
+    @pl.loop(last - FINAL_LAG + 1 + EARLY_FINALS, n)
     def _(step):
         final_stage(step)
 
@@ -364,6 +387,7 @@
                 pltpu.VMEM((4, num_batch * ROWS, dim), bf16),
                 pltpu.VMEM((CHUNK // 2, 64, span), f32),
                 pltpu.VMEM((CHUNK // 2, 64, 128), f32),
+                pltpu.VMEM((CHUNK // 2, 64, span), bf16),
                 pltpu.VMEM((n + 1, 2, CHUNK, ROWS, dim), f32),
                 pltpu.VMEM((n, 2, CHUNK, ROWS, dim), f32),
                 pltpu.VMEM((n + 1, 2, CHUNK, ROWS, dim), f32),
@@ -372,10 +396,10 @@
                 pltpu.VMEM((n + 1, CHUNK, ROWS, dim), f32),
                 pltpu.VMEM((n + 1, CHUNK * ROWS, dim), bf16),
                 pltpu.VMEM((n + 1, ROWS, dim), f32),
-                pltpu.VMEM((n, CHUNK * ROWS, dim), bf16),
-                pltpu.VMEM((n, ROWS, dim), f32),
+                pltpu.VMEM((n + 1, CHUNK * ROWS, dim), bf16),
                 pltpu.VMEM((n + 1, ROWS, dim), f32),
-                pltpu.VMEM((n, CHUNK * ROWS, dim), bf16),
+                pltpu.VMEM((n + 1, ROWS, dim), f32),
+                pltpu.VMEM((n + 1, CHUNK * ROWS, dim), bf16),
                 dma(RING),
                 dma(RING),
                 dma(1),

time: 38.5 us -> 37.2 us (0.966)
  Pallas kernels: 36.5 us -> 35.2 us
    pallas_call x1, Pallas kernels: 36.5 us -> 35.2 us  [group_step(): pl.pallas_call(functools.partial(kernel, n, dim ** (-0.5)), out_shape=jax...]
where the time goes in v10:
time: 37.2 us; the launch traced here: 37 us
  Pallas kernels  35.2 us (95%)
  local copies, waits for them, and re-layouts  1.87 us (5%)
    pallas_call x1, Pallas kernels, group_step(): pl.pallas_call(functools.partial(kernel, n, dim ** (-0.5)), out_shape=jax...  35.2 us
    unnamed x1, local copies, waits for them, and re-layouts  1.87 us

profile of v10, /device:TPU:0, one launch (start us, length us, event | category | flops | bytes accessed | tf_op | source)
XLA Modules:
  0.0 37.0 jit_solution(12264786699374298145)
XLA Ops:
  0.0 35.2 %shard_map.46 = bf16[2048,128]{1,0:T(8,128)(2,1)} custom-call(s32[256]{0:T(256)} %len_ref.1, bf16[2048,128]{1,0:T(8,128)(2,1)} %bitcast.3, bf16[256,512,128]{2,1,0:T(8,128)(2,1)} %k_hbm.1, bf16[256,512,128]{2,1,0:T(8,128)(2,1)} %v_hbm.1), custom_call_target="tpu_custom_call" | custom-call | tf_op jit(solution)/shard_map/pallas_call | solution.py:379
  35.2 1.9 %copy.6 = bf16[256,8,128]{2,1,0:T(8,128)(2,1)} copy(bf16[256,8,128]{2,1,0:T(8,128)(2,1)} %bitcast.2) | data formatting | bytes 1048576

commit v11 on v10

--- a/solution.py
+++ b/solution.py
@@ -30,7 +30,7 @@
     q_hbm,
     k_hbm,
     v_hbm,
-    out_hbm,
+    out_buf,
     kbuf,
     vbuf,
     qbuf,
@@ -48,7 +48,6 @@
     recv_out,
     recv_lse,
     own_lse,
-    out_buf,
     k_sem,
     v_sem,
     q_local,
@@ -66,7 +65,6 @@
     o_recv,
     l_send,
     l_recv,
-    out_sem,
 ):
     me = lax.axis_index("dup")
     chip, core = me // 2, lax.rem(me, 2)
@@ -113,11 +111,6 @@
 
     def give_lse(step):
         return remote(send_lse.at[step], recv_lse.at[step], l_send.at[step], l_recv.at[step], far)
-
-    def store_out(step):
-        return pltpu.make_async_copy(
-            out_buf.at[step], out_hbm.at[pl.ds(step * CHUNK * ROWS, CHUNK * ROWS)], out_sem.at[step]
-        )
 
     whole_q = pltpu.make_async_copy(q_hbm, qbuf.at[OWN], q_local.at[0])
     whole_q.start()
@@ -223,6 +216,7 @@
             send_out[step, pl.ds(16 * i, 16), :] = jnp.concatenate(far_out, 0).astype(jnp.bfloat16)
 
     def merge_final(step):
+        rows = lax.rem(step, n) * CHUNK * ROWS
         mine, theirs = own_lse[step], recv_lse[step]
         top = jnp.maximum(mine, theirs)
         w_a, w_b = jnp.exp2(mine - top), jnp.exp2(theirs - top)
@@ -234,7 +228,7 @@
             for h in range(2):
                 b = 2 * i + h
                 outs.append(w_a[:, b : b + 1] * own_out[step, b] + w_b[:, b : b + 1] * other[8 * h : 8 * h + 8])
-            out_buf[step, pl.ds(16 * i, 16), :] = jnp.concatenate(outs, 0).astype(jnp.bfloat16)
+            out_buf[pl.ds(pl.multiple_of(rows + 16 * i, 16), 16), :] = jnp.concatenate(outs, 0).astype(jnp.bfloat16)
 
     def await_peer(step):
         give_part(step).wait_recv()
@@ -251,7 +245,6 @@
     def final_stage(step):
         await_far(step)
         merge_final(step)
-        store_out(step).start()
 
     def attend(step, with_next):
         slot, next_slot = lax.rem(step, RING), lax.rem(step + 1, RING)
@@ -316,10 +309,6 @@
         def _():
             send_far(step - LAG)
 
-        @pl.when(step >= FINAL_LAG)
-        def _():
-            store_out(step - FINAL_LAG).start()
-
         @pl.when(step + 1 + RING < n)
         def _():
             load_k(step + 1 + RING, lax.rem(step + 1, RING)).start()
@@ -334,7 +323,6 @@
     merge_final(last - FINAL_LAG)
     merge_chip(last - LAG)
     attend(last, False)
-    store_out(last - FINAL_LAG).start()
     give_part(last).start()
     give_stat(last).start()
     send_far(last - LAG)
@@ -366,7 +354,6 @@
         give_stat(step).wait_send()
         give_out(step).wait_send()
         give_lse(step).wait_send()
-        store_out(step).wait()
 
 
 def solution(mesh):
@@ -378,9 +365,9 @@
         hbm = pl.BlockSpec(memory_space=pltpu.HBM)
         out = pl.pallas_call(
             functools.partial(kernel, n, dim**-0.5),
-            out_shape=jax.ShapeDtypeStruct((num_batch * ROWS, dim), bf16),
+            out_shape=pltpu.VMEM((num_batch * ROWS, dim), bf16),
             in_specs=[pl.BlockSpec(memory_space=pltpu.SMEM), hbm, hbm, hbm],
-            out_specs=hbm,
+            out_specs=pl.BlockSpec(memory_space=pltpu.VMEM),
             scratch_shapes=[
                 pltpu.VMEM((RING, CHUNK, span, dim), bf16),
                 pltpu.VMEM((RING, CHUNK, span, dim), bf16),
@@ -399,14 +386,13 @@
                 pltpu.VMEM((n + 1, CHUNK * ROWS, dim), bf16),
                 pltpu.VMEM((n + 1, ROWS, dim), f32),
                 pltpu.VMEM((n + 1, ROWS, dim), f32),
-                pltpu.VMEM((n + 1, CHUNK * ROWS, dim), bf16),
                 dma(RING),
                 dma(RING),
                 dma(1),
             ]
-            + [dma(n)] * 15,
+            + [dma(n)] * 14,
             compiler_params=pltpu.CompilerParams(
-                collective_id=0, has_side_effects=True, vmem_limit_bytes=60 * 1024 * 1024
+                collective_id=0, has_side_effects=True, vmem_limit_bytes=56 * 1024 * 1024
             ),
         )(len_local, q_local.reshape(num_batch * ROWS, dim), k_span, v_span)
         return out.reshape(num_batch, ROWS, dim)

time: 37.2 us -> 35.4 us (0.952)
  local copies, waits for them, and re-layouts: 1.87 us -> 0.8 us
  Pallas kernels: 35.2 us -> 34.5 us
    unnamed x1, local copies, waits for them, and re-layouts: 1.87 us -> 0.8 us
    pallas_call x1, Pallas kernels: 35.2 us -> 34.5 us  [group_step(): pl.pallas_call(functools.partial(kernel, n, dim ** (-0.5)), out_shape=plt...]
where the time goes in v11:
time: 35.4 us; the launch traced here: 35.3 us
  Pallas kernels  34.5 us (97%)
  local copies, waits for them, and re-layouts  0.8 us (2%)
    pallas_call x1, Pallas kernels, group_step(): pl.pallas_call(functools.partial(kernel, n, dim ** (-0.5)), out_shape=plt...  34.5 us
    unnamed x1, local copies, waits for them, and re-layouts  0.8 us

profile of v11, /device:TPU:0, one launch (start us, length us, event | category | flops | bytes accessed | tf_op | source)
XLA Modules:
  0.0 35.3 jit_solution(17571701784515288390)
XLA Ops:
  0.0 34.5 %shard_map.46 = bf16[2048,128]{1,0:T(8,128)(2,1)S(1)} custom-call(s32[256]{0:T(256)} %len_ref.1, bf16[2048,128]{1,0:T(8,128)(2,1)} %bitcast.3, bf16[256,512,128]{2,1,0:T(8,128)(2,1)} %k_hbm.1, bf16[256,512,128]{2,1,0:T(8,128)(2,1)} %v_hbm.1), custom_call_target="tpu_custom_call" | custom-call | tf_op jit(solution)/shard_map/pallas_call | solution.py:366
  34.5 0.8 %copy.6 = bf16[256,8,128]{2,1,0:T(8,128)(2,1)} copy(bf16[256,8,128]{2,1,0:T(8,128)(2,1)S(1)} %bitcast.2) | data formatting | bytes 1048576

commit v12 on v11

--- a/solution.py
+++ b/solution.py
@@ -114,7 +114,9 @@
 
     whole_q = pltpu.make_async_copy(q_hbm, qbuf.at[OWN], q_local.at[0])
     whole_q.start()
-    load_k(0, 0).start()
+    for step in range(2):
+        load_k(step, step).start()
+        load_v(step, step).start()
 
     barrier = pltpu.get_barrier_semaphore()
     for dev in (sib, far):
@@ -128,8 +130,7 @@
     def _(step):
         q_to_sib(step).start()
 
-    load_v(0, 0).start()
-    for step in range(1, RING):
+    for step in range(2, RING):
         load_k(step, step).start()
         load_v(step, step).start()
 
@@ -154,8 +155,13 @@
         start = pl.multiple_of(step * CHUNK * ROWS, 16) + 16 * i
         q = [qbuf[role, pl.ds(start, 16), :] for role in range(4)]
         left = jnp.concatenate([jnp.concatenate([x * of_first, x * of_second], 1) for x in q], 0)
-        right = jnp.concatenate([kbuf[slot, 2 * i], kbuf[slot, 2 * i + 1]], 1)
-        return lax.dot_general(left, right, (((1,), (1,)), ((), ())), preferred_element_type=jnp.float32)
+        k_a, k_b = kbuf[slot, 2 * i], kbuf[slot, 2 * i + 1]
+        turned = span // 2
+        right = jnp.concatenate([k_a[:turned], k_b[:turned]], 1)
+        scores = lax.dot_general(left, right, (((1,), (1,)), ((), ())), preferred_element_type=jnp.float32)
+        rest = jnp.concatenate([k_a[turned:].T, k_b[turned:].T], 0)
+        more = lax.dot_general(left, rest, (((1,), (0,)), ((), ())), preferred_element_type=jnp.float32)
+        return jnp.concatenate([scores, more], 1)
 
     def mask_pair(step, i, scores):
         for h in range(2):

time: 35.4 us -> 35.6 us (level)
  no operation moved by 1% of the time
where the time goes in v12:
time: 35.6 us; the launch traced here: 35.5 us
  Pallas kernels  34.7 us (97%)
  local copies, waits for them, and re-layouts  0.8 us (2%)
    pallas_call x1, Pallas kernels, group_step(): pl.pallas_call(functools.partial(kernel, n, dim ** (-0.5)), out_shape=plt...  34.7 us
    unnamed x1, local copies, waits for them, and re-layouts  0.8 us

profile of v12, /device:TPU:0, one launch (start us, length us, event | category | flops | bytes accessed | tf_op | source)
XLA Modules:
  0.0 35.5 jit_solution(3077200110218878075)
XLA Ops:
  0.0 34.7 %shard_map.46 = bf16[2048,128]{1,0:T(8,128)(2,1)S(1)} custom-call(s32[256]{0:T(256)} %len_ref.1, bf16[2048,128]{1,0:T(8,128)(2,1)} %bitcast.3, bf16[256,512,128]{2,1,0:T(8,128)(2,1)} %k_hbm.1, bf16[256,512,128]{2,1,0:T(8,128)(2,1)} %v_hbm.1), custom_call_target="tpu_custom_call" | custom-call | tf_op jit(solution)/shard_map/pallas_call | solution.py:372
  34.7 0.8 %copy.6 = bf16[256,8,128]{2,1,0:T(8,128)(2,1)} copy(bf16[256,8,128]{2,1,0:T(8,128)(2,1)S(1)} %bitcast.2) | data formatting | bytes 1048576

commit v13 on v12

--- a/solution.py
+++ b/solution.py
@@ -11,8 +11,8 @@
 DRAFT = 4
 CHUNK = 16
 RING = 6
-AHEAD = 2
-LAG = 2
+AHEAD = 4
+LAG = 3
 FINAL_LAG = 8
 EARLY_FINALS = 4
 PV_LAG = 2

time: 35.6 us -> 36.9 us (1.037)
  Pallas kernels: 34.7 us -> 36 us
    pallas_call x1, Pallas kernels: 34.7 us -> 36 us  [group_step(): pl.pallas_call(functools.partial(kernel, n, dim ** (-0.5)), out_shape=plt...]
where the time goes in v13:
time: 36.9 us; the launch traced here: 36.8 us
  Pallas kernels  36 us (98%)
  local copies, waits for them, and re-layouts  0.8 us (2%)
    pallas_call x1, Pallas kernels, group_step(): pl.pallas_call(functools.partial(kernel, n, dim ** (-0.5)), out_shape=plt...  36 us
    unnamed x1, local copies, waits for them, and re-layouts  0.8 us

profile of v13, /device:TPU:0, one launch (start us, length us, event | category | flops | bytes accessed | tf_op | source)
XLA Modules:
  0.0 36.8 jit_solution(9066407252545514864)
XLA Ops:
  0.0 36.0 %shard_map.46 = bf16[2048,128]{1,0:T(8,128)(2,1)S(1)} custom-call(s32[256]{0:T(256)} %len_ref.1, bf16[2048,128]{1,0:T(8,128)(2,1)} %bitcast.3, bf16[256,512,128]{2,1,0:T(8,128)(2,1)} %k_hbm.1, bf16[256,512,128]{2,1,0:T(8,128)(2,1)} %v_hbm.1), custom_call_target="tpu_custom_call" | custom-call | tf_op jit(solution)/shard_map/pallas_call | solution.py:372
  36.0 0.8 %copy.6 = bf16[256,8,128]{2,1,0:T(8,128)(2,1)} copy(bf16[256,8,128]{2,1,0:T(8,128)(2,1)S(1)} %bitcast.2) | data formatting | bytes 1048576

commit v14 on v12

--- a/solution.py
+++ b/solution.py
@@ -114,9 +114,7 @@
 
     whole_q = pltpu.make_async_copy(q_hbm, qbuf.at[OWN], q_local.at[0])
     whole_q.start()
-    for step in range(2):
-        load_k(step, step).start()
-        load_v(step, step).start()
+    load_k(0, 0).start()
 
     barrier = pltpu.get_barrier_semaphore()
     for dev in (sib, far):
@@ -130,7 +128,8 @@
     def _(step):
         q_to_sib(step).start()
 
-    for step in range(2, RING):
+    load_v(0, 0).start()
+    for step in range(1, RING):
         load_k(step, step).start()
         load_v(step, step).start()
 

time: 35.6 us -> 33.8 us (0.949)
  Pallas kernels: 34.7 us -> 32.9 us
    pallas_call x1, Pallas kernels: 34.7 us -> 32.9 us  [group_step(): pl.pallas_call(functools.partial(kernel, n, dim ** (-0.5)), out_shape=plt...]
where the time goes in v14:
time: 33.8 us; the launch traced here: 33.7 us
  Pallas kernels  32.9 us (97%)
  local copies, waits for them, and re-layouts  0.8 us (2%)
    pallas_call x1, Pallas kernels, group_step(): pl.pallas_call(functools.partial(kernel, n, dim ** (-0.5)), out_shape=plt...  32.9 us
    unnamed x1, local copies, waits for them, and re-layouts  0.8 us

profile of v14, /device:TPU:0, one launch (start us, length us, event | category | flops | bytes accessed | tf_op | source)
XLA Modules:
  0.0 33.7 jit_solution(3025489328591960386)
XLA Ops:
  0.0 32.9 %shard_map.46 = bf16[2048,128]{1,0:T(8,128)(2,1)S(1)} custom-call(s32[256]{0:T(256)} %len_ref.1, bf16[2048,128]{1,0:T(8,128)(2,1)} %bitcast.3, bf16[256,512,128]{2,1,0:T(8,128)(2,1)} %k_hbm.1, bf16[256,512,128]{2,1,0:T(8,128)(2,1)} %v_hbm.1), custom_call_target="tpu_custom_call" | custom-call | tf_op jit(solution)/shard_map/pallas_call | solution.py:371
  32.9 0.8 %copy.6 = bf16[256,8,128]{2,1,0:T(8,128)(2,1)} copy(bf16[256,8,128]{2,1,0:T(8,128)(2,1)S(1)} %bitcast.2) | data formatting | bytes 1048576

commit v15 on v14

--- a/solution.py
+++ b/solution.py
@@ -10,7 +10,7 @@
 
 DRAFT = 4
 CHUNK = 16
-RING = 6
+RING = 4
 AHEAD = 2
 LAG = 2
 FINAL_LAG = 8
@@ -129,9 +129,7 @@
         q_to_sib(step).start()
 
     load_v(0, 0).start()
-    for step in range(1, RING):
-        load_k(step, step).start()
-        load_v(step, step).start()
+    load_k(1, 1).start()
 
     def forward_q(step):
         q_to_far(step).wait_recv()
@@ -273,11 +271,14 @@
         forward_q(step)
         q_to_far(2 * step + 4).start()
         q_to_far(2 * step + 5).start()
+    load_v(1, 1).start()
+    load_k(2, 2).start()
     await_q(0)
     load_k(0, 0).wait()
     for i in range(pairs):
         mask_pair(0, i, score_pair(0, 0, i))
-    load_k(RING, 0).start()
+    load_v(2, 2).start()
+    load_k(3, 3).start()
 
     @pl.loop(0, last)
     def _(step):
@@ -289,6 +290,14 @@
         @pl.when(step + AHEAD < n)
         def _():
             forward_q(step + AHEAD)
+
+        @pl.when(step + RING < n)
+        def _():
+            load_k(step + RING, lax.rem(step, RING)).start()
+
+        @pl.when(step + RING - 1 < n)
+        def _():
+            load_v(step + RING - 1, lax.rem(step + RING - 1, RING)).start()
 
         await_q(step + 1)
         load_k(step + 1, lax.rem(step + 1, RING)).wait()
@@ -313,14 +322,6 @@
         @pl.when(step >= LAG)
         def _():
             send_far(step - LAG)
-
-        @pl.when(step + 1 + RING < n)
-        def _():
-            load_k(step + 1 + RING, lax.rem(step + 1, RING)).start()
-
-        @pl.when(step + RING < n)
-        def _():
-            load_v(step + RING, lax.rem(step, RING)).start()
 
     load_v(last, lax.rem(last, RING)).wait()
     await_peer(last - LAG)

time: 33.8 us -> 35.4 us (1.047)
  Pallas kernels: 32.9 us -> 34.5 us
    pallas_call x1, Pallas kernels: 32.9 us -> 34.5 us  [group_step(): pl.pallas_call(functools.partial(kernel, n, dim ** (-0.5)), out_shape=plt...]
where the time goes in v15:
time: 35.4 us; the launch traced here: 35.3 us
  Pallas kernels  34.5 us (97%)
  local copies, waits for them, and re-layouts  0.8 us (2%)
    pallas_call x1, Pallas kernels, group_step(): pl.pallas_call(functools.partial(kernel, n, dim ** (-0.5)), out_shape=plt...  34.5 us
    unnamed x1, local copies, waits for them, and re-layouts  0.8 us

profile of v15, /device:TPU:0, one launch (start us, length us, event | category | flops | bytes accessed | tf_op | source)
XLA Modules:
  0.0 35.3 jit_solution(16701442184614472241)
XLA Ops:
  0.0 34.5 %shard_map.46 = bf16[2048,128]{1,0:T(8,128)(2,1)S(1)} custom-call(s32[256]{0:T(256)} %len_ref.1, bf16[2048,128]{1,0:T(8,128)(2,1)} %bitcast.3, bf16[256,512,128]{2,1,0:T(8,128)(2,1)} %k_hbm.1, bf16[256,512,128]{2,1,0:T(8,128)(2,1)} %v_hbm.1), custom_call_target="tpu_custom_call" | custom-call | tf_op jit(solution)/shard_map/pallas_call | solution.py:372
  34.5 0.8 %copy.6 = bf16[256,8,128]{2,1,0:T(8,128)(2,1)} copy(bf16[256,8,128]{2,1,0:T(8,128)(2,1)S(1)} %bitcast.2) | data formatting | bytes 1048576

commit v16 on v14

--- a/solution.py
+++ b/solution.py
@@ -11,7 +11,7 @@
 DRAFT = 4
 CHUNK = 16
 RING = 6
-AHEAD = 2
+AHEAD = 3
 LAG = 2
 FINAL_LAG = 8
 EARLY_FINALS = 4
@@ -80,6 +80,12 @@
     def load_v(step, slot):
         return pltpu.make_async_copy(v_hbm.at[pl.ds(step * CHUNK, CHUNK)], vbuf.at[slot], v_sem.at[slot])
 
+    def refill(first, end):
+        for step in range(first, end):
+            load_v(step, step).start()
+            if step + 1 < RING:
+                load_k(step + 1, step + 1).start()
+
     def q_rows(step, role):
         return qbuf.at[role, pl.ds(step * CHUNK * ROWS, CHUNK * ROWS)]
 
@@ -128,10 +134,7 @@
     def _(step):
         q_to_sib(step).start()
 
-    load_v(0, 0).start()
-    for step in range(1, RING):
-        load_k(step, step).start()
-        load_v(step, step).start()
+    refill(0, 2)
 
     def forward_q(step):
         q_to_far(step).wait_recv()
@@ -269,12 +272,18 @@
         stat[step, 1] = masses
 
     last = n - 1
-    for step in range(AHEAD):
+    def start_q(step):
         forward_q(step)
         q_to_far(2 * step + 4).start()
         q_to_far(2 * step + 5).start()
+
+    start_q(0)
+    start_q(1)
+    refill(2, 3)
     await_q(0)
     load_k(0, 0).wait()
+    start_q(2)
+    refill(3, RING)
     for i in range(pairs):
         mask_pair(0, i, score_pair(0, 0, i))
     load_k(RING, 0).start()

time: 33.8 us -> 34.7 us (1.027)
  Pallas kernels: 32.9 us -> 33.8 us
    pallas_call x1, Pallas kernels: 32.9 us -> 33.8 us  [group_step(): pl.pallas_call(functools.partial(kernel, n, dim ** (-0.5)), out_shape=plt...]
where the time goes in v16:
time: 34.7 us; the launch traced here: 34.6 us
  Pallas kernels  33.8 us (97%)
  local copies, waits for them, and re-layouts  0.8 us (2%)
    pallas_call x1, Pallas kernels, group_step(): pl.pallas_call(functools.partial(kernel, n, dim ** (-0.5)), out_shape=plt...  33.8 us
    unnamed x1, local copies, waits for them, and re-layouts  0.8 us

profile of v16, /device:TPU:0, one launch (start us, length us, event | category | flops | bytes accessed | tf_op | source)
XLA Modules:
  0.0 34.6 jit_solution(2596106956247883355)
XLA Ops:
  0.0 33.8 %shard_map.46 = bf16[2048,128]{1,0:T(8,128)(2,1)S(1)} custom-call(s32[256]{0:T(256)} %len_ref.1, bf16[2048,128]{1,0:T(8,128)(2,1)} %bitcast.3, bf16[256,512,128]{2,1,0:T(8,128)(2,1)} %k_hbm.1, bf16[256,512,128]{2,1,0:T(8,128)(2,1)} %v_hbm.1), custom_call_target="tpu_custom_call" | custom-call | tf_op jit(solution)/shard_map/pallas_call | solution.py:380
  33.8 0.8 %copy.6 = bf16[256,8,128]{2,1,0:T(8,128)(2,1)} copy(bf16[256,8,128]{2,1,0:T(8,128)(2,1)S(1)} %bitcast.2) | data formatting | bytes 1048576

commit v17 on v14

--- a/solution.py
+++ b/solution.py
@@ -41,7 +41,6 @@
     give,
     peer,
     stat,
-    peer_stat,
     own_out,
     send_out,
     send_lse,
@@ -59,8 +58,6 @@
     q_fwd_recv,
     part_send,
     part_recv,
-    stat_send,
-    stat_recv,
     o_send,
     o_recv,
     l_send,
@@ -94,17 +91,13 @@
     def q_to_far(step):
         return remote(q_mine(step), q_rows(step, FAR), q_chip_send.at[step], q_chip_recv.at[step], far)
 
-    def q_to_sib(step):
-        return remote(q_mine(step), q_rows(step, SIB), q_sib_send.at[step], q_sib_recv.at[step], sib)
+    q_to_sib = remote(qbuf.at[OWN], qbuf.at[SIB], q_sib_send.at[0], q_sib_recv.at[0], sib)
 
     def q_forward(step):
         return remote(q_rows(step, FAR), q_rows(step, FAR_SIB), q_fwd_send.at[step], q_fwd_recv.at[step], sib)
 
     def give_part(step):
         return remote(give.at[step], peer.at[step], part_send.at[step], part_recv.at[step], sib)
-
-    def give_stat(step):
-        return remote(stat.at[step], peer_stat.at[step], stat_send.at[step], stat_recv.at[step], sib)
 
     def give_out(step):
         return remote(send_out.at[step], recv_out.at[step], o_send.at[step], o_recv.at[step], far)
@@ -121,13 +114,11 @@
         pl.semaphore_signal(barrier, inc=1, device_id={"dup": dev}, device_id_type=MESH)
     pl.semaphore_wait(barrier, 2)
     whole_q.wait()
-    for step in range(4):
+    @pl.loop(0, n)
+    def _(step):
         q_to_far(step).start()
 
-    @pl.loop(0, n)
-    def _(step):
-        q_to_sib(step).start()
-
+    q_to_sib.start()
     load_v(0, 0).start()
     for step in range(1, RING):
         load_k(step, step).start()
@@ -138,7 +129,6 @@
         q_forward(step).start()
 
     def await_q(step):
-        q_to_sib(step).wait_recv()
         q_forward(step).wait_recv()
 
     lane = lax.broadcasted_iota(jnp.int32, (ROWS, 128), 1)
@@ -194,11 +184,11 @@
         for h in range(2):
             for d in range(4):
                 home = keep if d in (OWN, FAR) else give
-                home[step, d % 2, 2 * i + h] = o[16 * d + 8 * h : 16 * d + 8 * h + 8, 128 * h : 128 * h + 128]
+                home[step, CHUNK * (d % 2) + 2 * i + h] = o[16 * d + 8 * h : 16 * d + 8 * h + 8, 128 * h : 128 * h + 128]
 
     def merge_chip(step):
         m_a, l_a = stat[step, 0], stat[step, 1]
-        m_b, l_b = (pltpu.roll(peer_stat[step, j], 128 - SIB * CHUNK, 1) for j in range(2))
+        m_b, l_b = (pltpu.roll(peer[step, 2 * CHUNK + j], 128 - SIB * CHUNK, 1) for j in range(2))
         top = jnp.maximum(m_a, m_b)
         w_a, w_b = jnp.exp2((m_a - top) * rate), jnp.exp2((m_b - top) * rate)
         total = w_a * l_a + w_b * l_b
@@ -212,7 +202,7 @@
 
         def both(role, b):
             c = role * CHUNK + b
-            return w_a[:, c : c + 1] * keep[step, role, b] + w_b[:, c : c + 1] * peer[step, role, b]
+            return w_a[:, c : c + 1] * keep[step, c] + w_b[:, c : c + 1] * peer[step, c]
 
         for i in range(pairs):
             for b in (2 * i, 2 * i + 1):
@@ -237,7 +227,6 @@
 
     def await_peer(step):
         give_part(step).wait_recv()
-        give_stat(step).wait_recv()
 
     def send_far(step):
         give_out(step).start()
@@ -267,12 +256,13 @@
                 mask_pair(step + 1, i - 1, scores[i - 1])
         stat[step, 0] = peaks
         stat[step, 1] = masses
+        give[step, 2 * CHUNK] = peaks
+        give[step, 2 * CHUNK + 1] = masses
 
     last = n - 1
     for step in range(AHEAD):
         forward_q(step)
-        q_to_far(2 * step + 4).start()
-        q_to_far(2 * step + 5).start()
+    q_to_sib.wait_recv()
     await_q(0)
     load_k(0, 0).wait()
     for i in range(pairs):
@@ -281,11 +271,6 @@
 
     @pl.loop(0, last)
     def _(step):
-        @pl.when(2 * step + 2 * AHEAD + 4 < n)
-        def _():
-            q_to_far(2 * step + 2 * AHEAD + 4).start()
-            q_to_far(2 * step + 2 * AHEAD + 5).start()
-
         @pl.when(step + AHEAD < n)
         def _():
             forward_q(step + AHEAD)
@@ -308,7 +293,6 @@
         merge_chip(ready * (step - LAG) + (1 - ready) * n)
         attend(step, True)
         give_part(step).start()
-        give_stat(step).start()
 
         @pl.when(step >= LAG)
         def _():
@@ -329,7 +313,6 @@
     merge_chip(last - LAG)
     attend(last, False)
     give_part(last).start()
-    give_stat(last).start()
     send_far(last - LAG)
 
     @pl.loop(last - LAG + 1, last)
@@ -350,13 +333,13 @@
     def _(step):
         final_stage(step)
 
+    q_to_sib.wait_send()
+
     @pl.loop(0, n)
     def _(step):
         q_to_far(step).wait_send()
-        q_to_sib(step).wait_send()
         q_forward(step).wait_send()
         give_part(step).wait_send()
-        give_stat(step).wait_send()
         give_out(step).wait_send()
         give_lse(step).wait_send()
 
@@ -380,10 +363,9 @@
                 pltpu.VMEM((CHUNK // 2, 64, span), f32),
                 pltpu.VMEM((CHUNK // 2, 64, 128), f32),
                 pltpu.VMEM((CHUNK // 2, 64, span), bf16),
-                pltpu.VMEM((n + 1, 2, CHUNK, ROWS, dim), f32),
-                pltpu.VMEM((n, 2, CHUNK, ROWS, dim), f32),
-                pltpu.VMEM((n + 1, 2, CHUNK, ROWS, dim), f32),
-                pltpu.VMEM((n + 1, 2, ROWS, dim), f32),
+                pltpu.VMEM((n + 1, 2 * CHUNK, ROWS, dim), f32),
+                pltpu.VMEM((n, 2 * CHUNK + 2, ROWS, dim), f32),
+                pltpu.VMEM((n + 1, 2 * CHUNK + 2, ROWS, dim), f32),
                 pltpu.VMEM((n + 1, 2, ROWS, dim), f32),
                 pltpu.VMEM((n + 1, CHUNK, ROWS, dim), f32),
                 pltpu.VMEM((n + 1, CHUNK * ROWS, dim), bf16),
@@ -395,7 +377,7 @@
                 dma(RING),
                 dma(1),
             ]
-            + [dma(n)] * 14,
+            + [dma(n)] * 12,
             compiler_params=pltpu.CompilerParams(
                 collective_id=0, has_side_effects=True, vmem_limit_bytes=56 * 1024 * 1024
             ),

time: 33.8 us -> 34.3 us (1.015)
  Pallas kernels: 32.9 us -> 33.4 us
    pallas_call x1, Pallas kernels: 32.9 us -> 33.4 us  [group_step(): pl.pallas_call(functools.partial(kernel, n, dim ** (-0.5)), out_shape=plt...]
where the time goes in v17:
time: 34.3 us; the launch traced here: 34.2 us
  Pallas kernels  33.4 us (97%)
  local copies, waits for them, and re-layouts  0.8 us (2%)
    pallas_call x1, Pallas kernels, group_step(): pl.pallas_call(functools.partial(kernel, n, dim ** (-0.5)), out_shape=plt...  33.4 us
    unnamed x1, local copies, waits for them, and re-layouts  0.8 us

profile of v17, /device:TPU:0, one launch (start us, length us, event | category | flops | bytes accessed | tf_op | source)
XLA Modules:
  0.0 34.2 jit_solution(8342894893360035373)
XLA Ops:
  0.0 33.4 %shard_map.46 = bf16[2048,128]{1,0:T(8,128)(2,1)S(1)} custom-call(s32[256]{0:T(256)} %len_ref.1, bf16[2048,128]{1,0:T(8,128)(2,1)} %bitcast.3, bf16[256,512,128]{2,1,0:T(8,128)(2,1)} %k_hbm.1, bf16[256,512,128]{2,1,0:T(8,128)(2,1)} %v_hbm.1), custom_call_target="tpu_custom_call" | custom-call | tf_op jit(solution)/shard_map/pallas_call | solution.py:354
  33.4 0.8 %copy.6 = bf16[256,8,128]{2,1,0:T(8,128)(2,1)} copy(bf16[256,8,128]{2,1,0:T(8,128)(2,1)S(1)} %bitcast.2) | data formatting | bytes 1048576

commit v18 on v17

--- a/solution.py
+++ b/solution.py
@@ -114,10 +114,8 @@
         pl.semaphore_signal(barrier, inc=1, device_id={"dup": dev}, device_id_type=MESH)
     pl.semaphore_wait(barrier, 2)
     whole_q.wait()
-    @pl.loop(0, n)
-    def _(step):
+    for step in range(4):
         q_to_far(step).start()
-
     q_to_sib.start()
     load_v(0, 0).start()
     for step in range(1, RING):
@@ -262,6 +260,8 @@
     last = n - 1
     for step in range(AHEAD):
         forward_q(step)
+        q_to_far(2 * step + 4).start()
+        q_to_far(2 * step + 5).start()
     q_to_sib.wait_recv()
     await_q(0)
     load_k(0, 0).wait()
@@ -271,6 +271,11 @@
 
     @pl.loop(0, last)
     def _(step):
+        @pl.when(2 * step + 2 * AHEAD + 4 < n)
+        def _():
+            q_to_far(2 * step + 2 * AHEAD + 4).start()
+            q_to_far(2 * step + 2 * AHEAD + 5).start()
+
         @pl.when(step + AHEAD < n)
         def _():
             forward_q(step + AHEAD)

time: 34.3 us -> 33.5 us (0.977)
  Pallas kernels: 33.4 us -> 32.6 us
    pallas_call x1, Pallas kernels: 33.4 us -> 32.6 us  [group_step(): pl.pallas_call(functools.partial(kernel, n, dim ** (-0.5)), out_shape=plt...]
where the time goes in v18:
time: 33.5 us; the launch traced here: 33.4 us
  Pallas kernels  32.6 us (97%)
  local copies, waits for them, and re-layouts  0.8 us (2%)
    pallas_call x1, Pallas kernels, group_step(): pl.pallas_call(functools.partial(kernel, n, dim ** (-0.5)), out_shape=plt...  32.6 us
    unnamed x1, local copies, waits for them, and re-layouts  0.8 us

profile of v18, /device:TPU:0, one launch (start us, length us, event | category | flops | bytes accessed | tf_op | source)
XLA Modules:
  0.0 33.4 jit_solution(9163354670851942398)
XLA Ops:
  0.0 32.6 %shard_map.46 = bf16[2048,128]{1,0:T(8,128)(2,1)S(1)} custom-call(s32[256]{0:T(256)} %len_ref.1, bf16[2048,128]{1,0:T(8,128)(2,1)} %bitcast.3, bf16[256,512,128]{2,1,0:T(8,128)(2,1)} %k_hbm.1, bf16[256,512,128]{2,1,0:T(8,128)(2,1)} %v_hbm.1), custom_call_target="tpu_custom_call" | custom-call | tf_op jit(solution)/shard_map/pallas_call | solution.py:359
  32.6 0.8 %copy.6 = bf16[256,8,128]{2,1,0:T(8,128)(2,1)} copy(bf16[256,8,128]{2,1,0:T(8,128)(2,1)S(1)} %bitcast.2) | data formatting | bytes 1048576

commit v19 on v18

--- a/solution.py
+++ b/solution.py
@@ -114,7 +114,7 @@
         pl.semaphore_signal(barrier, inc=1, device_id={"dup": dev}, device_id_type=MESH)
     pl.semaphore_wait(barrier, 2)
     whole_q.wait()
-    for step in range(4):
+    for step in range(2):
         q_to_far(step).start()
     q_to_sib.start()
     load_v(0, 0).start()
@@ -259,9 +259,11 @@
 
     last = n - 1
     for step in range(AHEAD):
+        q_to_far(step).wait_send()
+        q_to_far(step + 2).start()
         forward_q(step)
-        q_to_far(2 * step + 4).start()
-        q_to_far(2 * step + 5).start()
+    for step in range(4, 4 + 2 * AHEAD):
+        q_to_far(step).start()
     q_to_sib.wait_recv()
     await_q(0)
     load_k(0, 0).wait()
@@ -340,9 +342,12 @@
 
     q_to_sib.wait_send()
 
+    @pl.loop(AHEAD, n)
+    def _(step):
+        q_to_far(step).wait_send()
+
     @pl.loop(0, n)
     def _(step):
-        q_to_far(step).wait_send()
         q_forward(step).wait_send()
         give_part(step).wait_send()
         give_out(step).wait_send()

time: 33.5 us -> 34.5 us (1.030)
  Pallas kernels: 32.6 us -> 33.6 us
    pallas_call x1, Pallas kernels: 32.6 us -> 33.6 us  [group_step(): pl.pallas_call(functools.partial(kernel, n, dim ** (-0.5)), out_shape=plt...]
where the time goes in v19:
time: 34.5 us; the launch traced here: 34.4 us
  Pallas kernels  33.6 us (97%)
  local copies, waits for them, and re-layouts  0.8 us (2%)
    pallas_call x1, Pallas kernels, group_step(): pl.pallas_call(functools.partial(kernel, n, dim ** (-0.5)), out_shape=plt...  33.6 us
    unnamed x1, local copies, waits for them, and re-layouts  0.8 us

profile of v19, /device:TPU:0, one launch (start us, length us, event | category | flops | bytes accessed | tf_op | source)
XLA Modules:
  0.0 34.4 jit_solution(4905076275479068002)
XLA Ops:
  0.0 33.6 %shard_map.46 = bf16[2048,128]{1,0:T(8,128)(2,1)S(1)} custom-call(s32[256]{0:T(256)} %len_ref.1, bf16[2048,128]{1,0:T(8,128)(2,1)} %bitcast.3, bf16[256,512,128]{2,1,0:T(8,128)(2,1)} %k_hbm.1, bf16[256,512,128]{2,1,0:T(8,128)(2,1)} %v_hbm.1), custom_call_target="tpu_custom_call" | custom-call | tf_op jit(solution)/shard_map/pallas_call | solution.py:364
  33.6 0.8 %copy.6 = bf16[256,8,128]{2,1,0:T(8,128)(2,1)} copy(bf16[256,8,128]{2,1,0:T(8,128)(2,1)S(1)} %bitcast.2) | data formatting | bytes 1048576

commit v20 on v18

--- a/solution.py
+++ b/solution.py
@@ -15,7 +15,7 @@
 LAG = 2
 FINAL_LAG = 8
 EARLY_FINALS = 4
-PV_LAG = 2
+PV_LAG = 3
 ROWS = 8
 OWN, FAR, SIB, FAR_SIB = range(4)
 MESH = pl.DeviceIdType.MESH

time: 33.5 us -> 33.6 us (level)
  no operation moved by 1% of the time
where the time goes in v20:
time: 33.6 us; the launch traced here: 33.5 us
  Pallas kernels  32.7 us (97%)
  local copies, waits for them, and re-layouts  0.8 us (2%)
    pallas_call x1, Pallas kernels, group_step(): pl.pallas_call(functools.partial(kernel, n, dim ** (-0.5)), out_shape=plt...  32.7 us
    unnamed x1, local copies, waits for them, and re-layouts  0.8 us

profile of v20, /device:TPU:0, one launch (start us, length us, event | category | flops | bytes accessed | tf_op | source)
XLA Modules:
  0.0 33.5 jit_solution(7623027778551058987)
XLA Ops:
  0.0 32.7 %shard_map.46 = bf16[2048,128]{1,0:T(8,128)(2,1)S(1)} custom-call(s32[256]{0:T(256)} %len_ref.1, bf16[2048,128]{1,0:T(8,128)(2,1)} %bitcast.3, bf16[256,512,128]{2,1,0:T(8,128)(2,1)} %k_hbm.1, bf16[256,512,128]{2,1,0:T(8,128)(2,1)} %v_hbm.1), custom_call_target="tpu_custom_call" | custom-call | tf_op jit(solution)/shard_map/pallas_call | solution.py:359
  32.7 0.8 %copy.6 = bf16[256,8,128]{2,1,0:T(8,128)(2,1)} copy(bf16[256,8,128]{2,1,0:T(8,128)(2,1)S(1)} %bitcast.2) | data formatting | bytes 1048576

commit v21 on v18

--- a/solution.py
+++ b/solution.py
@@ -334,10 +334,6 @@
     merge_chip(last)
     send_far(last)
 
-    @pl.loop(last - FINAL_LAG + 1 + EARLY_FINALS, n)
-    def _(step):
-        final_stage(step)
-
     q_to_sib.wait_send()
 
     @pl.loop(0, n)
@@ -345,6 +341,18 @@
         q_to_far(step).wait_send()
         q_forward(step).wait_send()
         give_part(step).wait_send()
+
+    @pl.loop(0, last - 2)
+    def _(step):
+        give_out(step).wait_send()
+        give_lse(step).wait_send()
+
+    @pl.loop(last - FINAL_LAG + 1 + EARLY_FINALS, n)
+    def _(step):
+        final_stage(step)
+
+    @pl.loop(last - 2, n)
+    def _(step):
         give_out(step).wait_send()
         give_lse(step).wait_send()
 

time: 33.5 us -> 33.4 us (level)
  no operation moved by 1% of the time
where the time goes in v21:
time: 33.4 us; the launch traced here: 33.3 us
  Pallas kernels  32.5 us (97%)
  local copies, waits for them, and re-layouts  0.8 us (2%)
    pallas_call x1, Pallas kernels, group_step(): pl.pallas_call(functools.partial(kernel, n, dim ** (-0.5)), out_shape=plt...  32.5 us
    unnamed x1, local copies, waits for them, and re-layouts  0.8 us

profile of v21, /device:TPU:0, one launch (start us, length us, event | category | flops | bytes accessed | tf_op | source)
XLA Modules:
  0.0 33.3 jit_solution(3989766607784943946)
XLA Ops:
  0.0 32.5 %shard_map.46 = bf16[2048,128]{1,0:T(8,128)(2,1)S(1)} custom-call(s32[256]{0:T(256)} %len_ref.1, bf16[2048,128]{1,0:T(8,128)(2,1)} %bitcast.3, bf16[256,512,128]{2,1,0:T(8,128)(2,1)} %k_hbm.1, bf16[256,512,128]{2,1,0:T(8,128)(2,1)} %v_hbm.1), custom_call_target="tpu_custom_call" | custom-call | tf_op jit(solution)/shard_map/pallas_call | solution.py:367
  32.5 0.8 %copy.6 = bf16[256,8,128]{2,1,0:T(8,128)(2,1)} copy(bf16[256,8,128]{2,1,0:T(8,128)(2,1)S(1)} %bitcast.2) | data formatting | bytes 1048576
